TPU v7x, 32 devices: a whole 2x2x4 slice. The times are simulated.
32 devices in a mesh: rep: 8 (over y, x, core), shard: 4 (over z).
Axes of the slice: x: 2, y: 2, z: 4, core: 2. Of those that a mesh axis runs over, the one named last changes fastest.
Arguments:
- layer_input: bfloat16 [8192, 1024], P(('rep', 'shard')), may hold values from -6 to 6
- query_weight: bfloat16 [1024, 1024], P('shard'), may hold values from -0.1875 to 0.1875
- query_bias: bfloat16 [1024], P('shard'), may hold values from -3 to 3
- key_weight: bfloat16 [1024, 1024], P('shard'), may hold values from -0.1875 to 0.1875
- key_bias: bfloat16 [1024], P('shard'), may hold values from -3 to 3
- value_weight: bfloat16 [1024, 1024], P('shard'), may hold values from -0.1875 to 0.1875
- value_bias: bfloat16 [1024], P('shard'), may hold values from -3 to 3
- output_weight: bfloat16 [1024, 1024], P('shard'), may hold values from -0.75 to 0.75
- output_bias: bfloat16 [1024], P('shard'), may hold values from -2.5 to 2.5
- up_weight: bfloat16 [1024, 4096], P('shard'), may hold values from -0.1875 to 0.1875
- up_bias: bfloat16 [4096], P('shard'), may hold values from -3 to 3
- down_weight: bfloat16 [4096, 1024], P('shard'), may hold values from -0.09375 to 0.09375
- down_bias: bfloat16 [1024], P('shard'), may hold values from -1.1953125 to 1.1953125
- attention_gain_in: bfloat16 [1024], P('shard'), may hold values from 0.25 to 1.75
- attention_gain_out: bfloat16 [1024], P('shard'), may hold values from 0.25 to 1.75
- feedforward_gain_in: bfloat16 [1024], P('shard'), may hold values from 0.25 to 1.75
- feedforward_gain_out: bfloat16 [1024], P('shard'), may hold values from 0.25 to 1.75
- layer_cotangent: bfloat16 [8192, 1024], P(('rep', 'shard')), may hold values from -6 to 6
Outputs:
- layer_output: bfloat16 [8192, 1024], P(('rep', 'shard'))
- input_gradient: float32 [8192, 1024], P(('rep', 'shard'))
- query_weight_gradient: float32 [1024, 1024], P('shard')
- query_bias_gradient: float32 [1024], P('shard')
- key_weight_gradient: float32 [1024, 1024], P('shard')
- key_bias_gradient: float32 [1024], P('shard')
- value_weight_gradient: float32 [1024, 1024], P('shard')
- value_bias_gradient: float32 [1024], P('shard')
- output_weight_gradient: float32 [1024, 1024], P('shard')
- output_bias_gradient: float32 [1024], P('shard')
- up_weight_gradient: float32 [1024, 4096], P('shard')
- up_bias_gradient: float32 [4096], P('shard')
- down_weight_gradient: float32 [4096, 1024], P('shard')
- down_bias_gradient: float32 [1024], P('shard')
- attention_gain_in_gradient: float32 [1024], P('shard')
- attention_gain_out_gradient: float32 [1024], P('shard')
- feedforward_gain_in_gradient: float32 [1024], P('shard')
- feedforward_gain_out_gradient: float32 [1024], P('shard')
All inputs are finite; a program needn't handle non-finite values.
Results may differ from a plain program's by a relative error of at most 0.03.
Values may be sent and summed in bfloat16 or wider, within the bound.
No kernel may reach another device: no remote copies, remote signals or barrier semaphores. Data moves between devices by JAX's collectives and lax.ppermute only.
A program may use at most 256 MiB of HBM per device.

v0:
```python
import math

import jax
import jax.numpy as jnp
from jax import lax
from jax.sharding import PartitionSpec as P

HEADS = 16


norm_epsilon = 1e-05


def normalize(values):
    centered = values - jnp.mean(values, axis=-1, keepdims=True)
    inverse = lax.rsqrt(jnp.mean(centered * centered, axis=-1, keepdims=True) + norm_epsilon)
    return (centered * inverse, inverse)


def norm_back(normed, inverse, upstream):
    return inverse * (
        upstream
        - jnp.mean(upstream, axis=-1, keepdims=True)
        - normed * jnp.mean(upstream * normed, axis=-1, keepdims=True)
    )


def rotation(positions, head_dim):
    half_dim = head_dim // 2
    freqs = 10000.0 ** (-jnp.arange(half_dim, dtype=jnp.float32) / half_dim)
    angles = positions.astype(jnp.float32)[:, None] * freqs[None, :]
    return (jnp.cos(angles)[:, None, :], jnp.sin(angles)[:, None, :])


def rotate(tensor, cosines, sines, sign):
    half_dim = tensor.shape[-1] // 2
    first = tensor[..., :half_dim]
    second = tensor[..., half_dim:]
    return jnp.concatenate(
        [first * cosines - sign * second * sines, second * cosines + sign * first * sines], axis=-1
    )


def col_sum(values):
    return jnp.sum(values.astype(jnp.float32), axis=0)


def per_device(
    layer_input,
    query_weight,
    query_bias,
    key_weight,
    key_bias,
    value_weight,
    value_bias,
    output_weight,
    output_bias,
    up_weight,
    up_bias,
    down_weight,
    down_bias,
    attention_gain_in,
    attention_gain_out,
    feedforward_gain_in,
    feedforward_gain_out,
    layer_cotangent,
):
    rows = layer_input.shape[0]
    width = layer_input.shape[1]
    heads = HEADS
    head_dim = width // heads
    seq_rows = rows * lax.axis_size("shard")
    factor = head_dim ** (-0.5)
    positions = lax.axis_index("shard") * rows + jnp.arange(rows, dtype=jnp.int32)
    cosines, sines = rotation(positions, head_dim)
    attention_local = (
        query_weight,
        key_weight,
        value_weight,
        output_weight,
        query_bias,
        key_bias,
        value_bias,
        output_bias,
        attention_gain_in,
        attention_gain_out,
    )
    feed_local = (
        up_weight,
        up_bias,
        down_weight,
        down_bias,
        feedforward_gain_in,
        feedforward_gain_out,
    )
    attention_full = (
        lax.all_gather(attention_local[0], "shard", axis=0, tiled=True),
        lax.all_gather(attention_local[1], "shard", axis=0, tiled=True),
        lax.all_gather(attention_local[2], "shard", axis=0, tiled=True),
        lax.all_gather(attention_local[3], "shard", axis=0, tiled=True),
        lax.all_gather(attention_local[4], "shard", axis=0, tiled=True),
        lax.all_gather(attention_local[5], "shard", axis=0, tiled=True),
        lax.all_gather(attention_local[6], "shard", axis=0, tiled=True),
        lax.all_gather(attention_local[7], "shard", axis=0, tiled=True),
        lax.all_gather(attention_local[8], "shard", axis=0, tiled=True),
        lax.all_gather(attention_local[9], "shard", axis=0, tiled=True),
    )
    (
        query_mat,
        key_mat,
        value_mat,
        out_mat,
        query_shift,
        key_shift,
        value_shift,
        out_shift,
        gain_in_a,
        gain_out_a,
    ) = attention_full
    residual_in = layer_input.astype(jnp.float32)
    normed_a, inverse_a = normalize(residual_in)
    hidden_a = (normed_a * gain_in_a.astype(jnp.float32)).astype(jnp.bfloat16)

    def project(matrix, shift):
        return jnp.dot(hidden_a, matrix, preferred_element_type=jnp.float32) + shift.astype(
            jnp.float32
        )

    query_heads = rotate(
        project(query_mat, query_shift).reshape(rows, heads, head_dim), cosines, sines, 1.0
    ).astype(jnp.bfloat16)
    key_rows = (
        rotate(project(key_mat, key_shift).reshape(rows, heads, head_dim), cosines, sines, 1.0)
        .astype(jnp.bfloat16)
        .reshape(rows, width)
    )
    value_rows = project(value_mat, value_shift).astype(jnp.bfloat16)
    start_state = (
        jnp.full((heads, rows), -1e30, jnp.float32),
        jnp.zeros((heads, rows), jnp.float32),
        jnp.zeros((heads, rows, head_dim), jnp.float32),
    )
    key_piece = lax.all_gather(key_rows, "shard", axis=0, tiled=True)
    value_piece = lax.all_gather(value_rows, "shard", axis=0, tiled=True)
    count = key_piece.shape[0]
    block = math.gcd(count, 512)

    def forward_inner(index, state):
        best, total, accum = state
        offset = index * block
        key_block = lax.dynamic_slice_in_dim(key_piece, offset, block, 0).reshape(
            block, heads, head_dim
        )
        value_block = lax.dynamic_slice_in_dim(value_piece, offset, block, 0).reshape(
            block, heads, head_dim
        )
        key_pos = offset + jnp.arange(block, dtype=jnp.int32)
        allowed = key_pos[None, None, :] <= positions[None, :, None]
        scores = (
            jnp.einsum("qhd,khd->hqk", query_heads, key_block, preferred_element_type=jnp.float32)
            * factor
        )
        scores = jnp.where(allowed, scores, -1e30)
        newest = jnp.maximum(best, jnp.max(scores, axis=-1))
        weights = jnp.where(allowed, jnp.exp(scores - newest[..., None]), 0.0)
        decay = jnp.exp(best - newest)
        total = total * decay + jnp.sum(weights, axis=-1)
        accum = accum * decay[..., None] + jnp.einsum(
            "hqk,khd->hqd",
            weights.astype(jnp.bfloat16),
            value_block,
            preferred_element_type=jnp.float32,
        )
        return (newest, total, accum)

    best, total, accum = lax.fori_loop(0, count // block, forward_inner, start_state)
    logsum = best + jnp.log(total)
    attended = (
        jnp.transpose(accum / total[..., None], (1, 0, 2)).reshape(rows, width).astype(jnp.bfloat16)
    )
    branch_a = jnp.dot(attended, out_mat, preferred_element_type=jnp.float32) + out_shift.astype(
        jnp.float32
    )
    normed_o, inverse_o = normalize(branch_a)
    middle = residual_in + normed_o * gain_out_a.astype(jnp.float32)
    feed_full = (
        lax.all_gather(feed_local[0], "shard", axis=0, tiled=True),
        lax.all_gather(feed_local[1], "shard", axis=0, tiled=True),
        lax.all_gather(feed_local[2], "shard", axis=0, tiled=True),
        lax.all_gather(feed_local[3], "shard", axis=0, tiled=True),
        lax.all_gather(feed_local[4], "shard", axis=0, tiled=True),
        lax.all_gather(feed_local[5], "shard", axis=0, tiled=True),
    )
    up_mat, up_shift, down_mat, down_shift, gain_in_f, gain_out_f = feed_full
    normed_f, inverse_f = normalize(middle)
    hidden_f = (normed_f * gain_in_f.astype(jnp.float32)).astype(jnp.bfloat16)
    pre_act = jnp.dot(hidden_f, up_mat, preferred_element_type=jnp.float32) + up_shift.astype(
        jnp.float32
    )
    activated = jax.nn.gelu(pre_act).astype(jnp.bfloat16)
    branch_f = jnp.dot(activated, down_mat, preferred_element_type=jnp.float32) + down_shift.astype(
        jnp.float32
    )
    normed_d, inverse_d = normalize(branch_f)
    layer_output = (middle + normed_d * gain_out_f.astype(jnp.float32)).astype(jnp.bfloat16)
    feed_back = (
        lax.all_gather(feed_local[0], "shard", axis=0, tiled=True),
        lax.all_gather(feed_local[1], "shard", axis=0, tiled=True),
        lax.all_gather(feed_local[2], "shard", axis=0, tiled=True),
        lax.all_gather(feed_local[3], "shard", axis=0, tiled=True),
        lax.all_gather(feed_local[4], "shard", axis=0, tiled=True),
        lax.all_gather(feed_local[5], "shard", axis=0, tiled=True),
    )
    up_back, up_unused, down_back, down_unused, gain_in_fb, gain_out_fb = feed_back
    upstream = layer_cotangent.astype(jnp.float32)
    grad_gain_out_f = jnp.sum(upstream * normed_d, axis=0)
    d_branch_f = norm_back(normed_d, inverse_d, upstream * gain_out_fb.astype(jnp.float32)).astype(
        jnp.bfloat16
    )
    grad_down = jnp.einsum("tf,td->fd", activated, d_branch_f, preferred_element_type=jnp.float32)
    grad_down_shift = col_sum(d_branch_f)
    d_activated = jnp.einsum("td,fd->tf", d_branch_f, down_back, preferred_element_type=jnp.float32)
    gelu_out, gelu_pull = jax.vjp(jax.nn.gelu, pre_act)
    d_pre = gelu_pull(d_activated)[0].astype(jnp.bfloat16)
    grad_up = jnp.einsum("td,tf->df", hidden_f, d_pre, preferred_element_type=jnp.float32)
    grad_up_shift = col_sum(d_pre)
    d_hidden_f = jnp.einsum("tf,df->td", d_pre, up_back, preferred_element_type=jnp.float32)
    grad_gain_in_f = jnp.sum(d_hidden_f * normed_f, axis=0)
    d_middle = upstream + norm_back(
        normed_f, inverse_f, d_hidden_f * gain_in_fb.astype(jnp.float32)
    )
    feed_grads = (
        lax.psum_scatter(
            grad_up.astype(jnp.bfloat16), "shard", scatter_dimension=0, tiled=True
        ).astype(jnp.float32),
        lax.psum_scatter(
            grad_up_shift.astype(jnp.bfloat16), "shard", scatter_dimension=0, tiled=True
        ).astype(jnp.float32),
        lax.psum_scatter(
            grad_down.astype(jnp.bfloat16), "shard", scatter_dimension=0, tiled=True
        ).astype(jnp.float32),
        lax.psum_scatter(
            grad_down_shift.astype(jnp.bfloat16), "shard", scatter_dimension=0, tiled=True
        ).astype(jnp.float32),
        lax.psum_scatter(
            grad_gain_in_f.astype(jnp.bfloat16), "shard", scatter_dimension=0, tiled=True
        ).astype(jnp.float32),
        lax.psum_scatter(
            grad_gain_out_f.astype(jnp.bfloat16), "shard", scatter_dimension=0, tiled=True
        ).astype(jnp.float32),
    )
    attention_back = (
        lax.all_gather(attention_local[0], "shard", axis=0, tiled=True),
        lax.all_gather(attention_local[1], "shard", axis=0, tiled=True),
        lax.all_gather(attention_local[2], "shard", axis=0, tiled=True),
        lax.all_gather(attention_local[3], "shard", axis=0, tiled=True),
        lax.all_gather(attention_local[4], "shard", axis=0, tiled=True),
        lax.all_gather(attention_local[5], "shard", axis=0, tiled=True),
        lax.all_gather(attention_local[6], "shard", axis=0, tiled=True),
        lax.all_gather(attention_local[7], "shard", axis=0, tiled=True),
        lax.all_gather(attention_local[8], "shard", axis=0, tiled=True),
        lax.all_gather(attention_local[9], "shard", axis=0, tiled=True),
    )
    (
        query_back,
        key_back,
        value_back,
        out_back,
        qshift_unused,
        kshift_unused,
        vshift_unused,
        oshift_unused,
        gain_in_ab,
        gain_out_ab,
    ) = attention_back
    grad_gain_out_a = jnp.sum(d_middle * normed_o, axis=0)
    d_branch_a = norm_back(normed_o, inverse_o, d_middle * gain_out_ab.astype(jnp.float32)).astype(
        jnp.bfloat16
    )
    grad_out_mat = jnp.einsum("td,te->de", attended, d_branch_a, preferred_element_type=jnp.float32)
    grad_out_shift = col_sum(d_branch_a)
    d_attended = jnp.einsum(
        "te,de->td", d_branch_a, out_back, preferred_element_type=jnp.float32
    ).astype(jnp.bfloat16)
    d_heads = d_attended.reshape(rows, heads, head_dim)
    row_delta = jnp.einsum(
        "qhd,qhd->hq",
        d_heads.astype(jnp.float32),
        attended.reshape(rows, heads, head_dim).astype(jnp.float32),
    )

    def query_terms(key_block, value_block, key_pos):
        allowed = key_pos[None, None, :] <= positions[None, :, None]
        scores = (
            jnp.einsum("qhd,khd->hqk", query_heads, key_block, preferred_element_type=jnp.float32)
            * factor
        )
        probs = jnp.where(allowed, jnp.exp(scores - logsum[..., None]), 0.0)
        d_probs = jnp.einsum(
            "qhd,khd->hqk", d_heads, value_block, preferred_element_type=jnp.float32
        )
        d_scores = (probs * (d_probs - row_delta[..., None])).astype(jnp.bfloat16)
        return (probs, d_scores)

    back_state = (
        jnp.zeros((rows, heads, head_dim), jnp.float32),
        jnp.zeros((seq_rows, width), jnp.float32),
        jnp.zeros((seq_rows, width), jnp.float32),
    )
    backward_key_piece = lax.all_gather(key_rows, "shard", axis=0, tiled=True)
    backward_value_piece = lax.all_gather(value_rows, "shard", axis=0, tiled=True)
    count = backward_key_piece.shape[0]
    backward_block = math.gcd(count, 512)

    def backward_inner(index, state):
        grad_query, grad_keys, grad_values = state
        offset = index * backward_block
        key_block = lax.dynamic_slice_in_dim(backward_key_piece, offset, backward_block, 0).reshape(
            backward_block, heads, head_dim
        )
        value_block = lax.dynamic_slice_in_dim(
            backward_value_piece, offset, backward_block, 0
        ).reshape(backward_block, heads, head_dim)
        key_pos = offset + jnp.arange(backward_block, dtype=jnp.int32)
        probs, d_scores = query_terms(key_block, value_block, key_pos)
        grad_query = (
            grad_query
            + jnp.einsum("hqk,khd->qhd", d_scores, key_block, preferred_element_type=jnp.float32)
            * factor
        )
        key_grad = (
            jnp.einsum("hqk,qhd->khd", d_scores, query_heads, preferred_element_type=jnp.float32)
            * factor
        )
        value_grad = jnp.einsum(
            "hqk,qhd->khd", probs.astype(jnp.bfloat16), d_heads, preferred_element_type=jnp.float32
        )
        grad_keys = lax.dynamic_update_slice_in_dim(
            grad_keys, key_grad.reshape(backward_block, width), offset, 0
        )
        grad_values = lax.dynamic_update_slice_in_dim(
            grad_values, value_grad.reshape(backward_block, width), offset, 0
        )
        return (grad_query, grad_keys, grad_values)

    back_result = lax.fori_loop(0, count // backward_block, backward_inner, back_state)
    grad_query = back_result[0]
    key_total, value_total = (
        lax.psum_scatter(
            back_result[1].astype(jnp.bfloat16), "shard", scatter_dimension=0, tiled=True
        ).astype(jnp.float32),
        lax.psum_scatter(
            back_result[2].astype(jnp.bfloat16), "shard", scatter_dimension=0, tiled=True
        ).astype(jnp.float32),
    )
    d_query = rotate(grad_query, cosines, sines, -1.0).reshape(rows, width).astype(jnp.bfloat16)
    d_key = (
        rotate(key_total.reshape(rows, heads, head_dim), cosines, sines, -1.0)
        .reshape(rows, width)
        .astype(jnp.bfloat16)
    )
    d_value = value_total.astype(jnp.bfloat16)
    grad_query_mat = jnp.einsum("td,te->de", hidden_a, d_query, preferred_element_type=jnp.float32)
    grad_key_mat = jnp.einsum("td,te->de", hidden_a, d_key, preferred_element_type=jnp.float32)
    grad_value_mat = jnp.einsum("td,te->de", hidden_a, d_value, preferred_element_type=jnp.float32)
    d_hidden_a = jnp.einsum("te,de->td", d_query, query_back, preferred_element_type=jnp.float32)
    d_hidden_a = d_hidden_a + jnp.einsum(
        "te,de->td", d_key, key_back, preferred_element_type=jnp.float32
    )
    d_hidden_a = d_hidden_a + jnp.einsum(
        "te,de->td", d_value, value_back, preferred_element_type=jnp.float32
    )
    grad_gain_in_a = jnp.sum(d_hidden_a * normed_a, axis=0)
    input_gradient = d_middle + norm_back(
        normed_a, inverse_a, d_hidden_a * gain_in_ab.astype(jnp.float32)
    )
    attention_grads = (
        lax.psum_scatter(
            grad_query_mat.astype(jnp.bfloat16), "shard", scatter_dimension=0, tiled=True
        ).astype(jnp.float32),
        lax.psum_scatter(
            grad_key_mat.astype(jnp.bfloat16), "shard", scatter_dimension=0, tiled=True
        ).astype(jnp.float32),
        lax.psum_scatter(
            grad_value_mat.astype(jnp.bfloat16), "shard", scatter_dimension=0, tiled=True
        ).astype(jnp.float32),
        lax.psum_scatter(
            grad_out_mat.astype(jnp.bfloat16), "shard", scatter_dimension=0, tiled=True
        ).astype(jnp.float32),
        lax.psum_scatter(
            col_sum(d_query).astype(jnp.bfloat16), "shard", scatter_dimension=0, tiled=True
        ).astype(jnp.float32),
        lax.psum_scatter(
            col_sum(d_key).astype(jnp.bfloat16), "shard", scatter_dimension=0, tiled=True
        ).astype(jnp.float32),
        lax.psum_scatter(
            col_sum(d_value).astype(jnp.bfloat16), "shard", scatter_dimension=0, tiled=True
        ).astype(jnp.float32),
        lax.psum_scatter(
            grad_out_shift.astype(jnp.bfloat16), "shard", scatter_dimension=0, tiled=True
        ).astype(jnp.float32),
        lax.psum_scatter(
            grad_gain_in_a.astype(jnp.bfloat16), "shard", scatter_dimension=0, tiled=True
        ).astype(jnp.float32),
        lax.psum_scatter(
            grad_gain_out_a.astype(jnp.bfloat16), "shard", scatter_dimension=0, tiled=True
        ).astype(jnp.float32),
    )
    (
        g_query,
        g_key,
        g_value,
        g_out,
        g_qshift,
        g_kshift,
        g_vshift,
        g_oshift,
        g_gain_in_a,
        g_gain_out_a,
    ) = attention_grads
    g_up, g_up_shift, g_down, g_down_shift, g_gain_in_f, g_gain_out_f = feed_grads
    summed = (
        lax.psum(g_query.astype(jnp.bfloat16), "rep").astype(jnp.float32),
        lax.psum(g_qshift.astype(jnp.bfloat16), "rep").astype(jnp.float32),
        lax.psum(g_key.astype(jnp.bfloat16), "rep").astype(jnp.float32),
        lax.psum(g_kshift.astype(jnp.bfloat16), "rep").astype(jnp.float32),
        lax.psum(g_value.astype(jnp.bfloat16), "rep").astype(jnp.float32),
        lax.psum(g_vshift.astype(jnp.bfloat16), "rep").astype(jnp.float32),
        lax.psum(g_out.astype(jnp.bfloat16), "rep").astype(jnp.float32),
        lax.psum(g_oshift.astype(jnp.bfloat16), "rep").astype(jnp.float32),
        lax.psum(g_up.astype(jnp.bfloat16), "rep").astype(jnp.float32),
        lax.psum(g_up_shift.astype(jnp.bfloat16), "rep").astype(jnp.float32),
        lax.psum(g_down.astype(jnp.bfloat16), "rep").astype(jnp.float32),
        lax.psum(g_down_shift.astype(jnp.bfloat16), "rep").astype(jnp.float32),
        lax.psum(g_gain_in_a.astype(jnp.bfloat16), "rep").astype(jnp.float32),
        lax.psum(g_gain_out_a.astype(jnp.bfloat16), "rep").astype(jnp.float32),
        lax.psum(g_gain_in_f.astype(jnp.bfloat16), "rep").astype(jnp.float32),
        lax.psum(g_gain_out_f.astype(jnp.bfloat16), "rep").astype(jnp.float32),
    )
    return (
        layer_output,
        input_gradient,
        summed[0],
        summed[1],
        summed[2],
        summed[3],
        summed[4],
        summed[5],
        summed[6],
        summed[7],
        summed[8],
        summed[9],
        summed[10],
        summed[11],
        summed[12],
        summed[13],
        summed[14],
        summed[15],
    )


def solution(mesh):
    return jax.shard_map(
        per_device,
        mesh=mesh,
        in_specs=(
            P(("rep", "shard"), None),
            P("shard", None),
            P("shard"),
            P("shard", None),
            P("shard"),
            P("shard", None),
            P("shard"),
            P("shard", None),
            P("shard"),
            P("shard", None),
            P("shard"),
            P("shard", None),
            P("shard"),
            P("shard"),
            P("shard"),
            P("shard"),
            P("shard"),
            P(("rep", "shard"), None),
        ),
        out_specs=(
            P(("rep", "shard"), None),
            P(("rep", "shard"), None),
            P("shard", None),
            P("shard"),
            P("shard", None),
            P("shard"),
            P("shard", None),
            P("shard"),
            P("shard", None),
            P("shard"),
            P("shard", None),
            P("shard"),
            P("shard", None),
            P("shard"),
            P("shard"),
            P("shard"),
            P("shard"),
            P("shard"),
        ),
        check_vma=False,
    )
```

profile of v0, /device:TPU:0, one launch (start us, length us, event | category | flops | bytes accessed | tf_op | source)
XLA Modules:
  0.0 1362.6 jit_solution(2872915875841751153)
XLA Ops:
  10.1 12.6 all-gather
  33.7 24.7 %all-gather.24.cloned.1.call-done = bf16[1024,1024]{1,0:T(8,128)(2,1)} async-done(((bf16[256,1024]{1,0:T(8,128)(2,1)}), bf16[1024,1024]{1,0:T(8,128)(2,1)}) %all-gather.24.cloned.1.call-update) | async-done | bytes 2097168 | tf_op jit(solution)/shard_map/all_gather | solution.py:99
  61.8 8.8 all-gather.2
  80.0 24.6 %all-gather.22.cloned.1.call-done = bf16[1024,1024]{1,0:T(8,128)(2,1)} async-done(((bf16[256,1024]{1,0:T(8,128)(2,1)}), bf16[1024,1024]{1,0:T(8,128)(2,1)}) %all-gather.22.cloned.1.call-update) | async-done | bytes 2097168 | tf_op jit(solution)/shard_map/all_gather | solution.py:97
  107.3 43.6 %all-gather.18.cloned.1.call-done = bf16[1024,1024]{1,0:T(8,128)(2,1)} async-done(((bf16[256,1024]{1,0:T(8,128)(2,1)}), bf16[1024,1024]{1,0:T(8,128)(2,1)}) %all-gather.18.cloned.1.call-update) | async-done | bytes 2097168 | tf_op jit(solution)/shard_map/all_gather | solution.py:98
  159.2 8.8 all-gather.7
  168.0 12.1 all_gather.80
  180.1 9.2 all-gather.5
  218.0 27.0 %all-gather.20.cloned.1.call-done = bf16[1024,1024]{0,1:T(8,128)(2,1)} async-done(((bf16[256,1024]{0,1:T(8,128)(2,1)}), bf16[1024,1024]{0,1:T(8,128)(2,1)}) %all-gather.20.cloned.1.call-update) | async-done | bytes 2097168 | tf_op jit(solution)/shard_map/all_gather | solution.py:143
  245.0 35.8 %while.36 = (s32[]{:T(128)}, f32[16,256]{1,0:T(8,128)S(1)}, f32[16,256]{1,0:T(8,128)S(1)}, f32[16,256,64]{1,2,0:T(8,128)}, bf16[1024,1024]{0,1:T(8,128)(2,1)}, /...) while((s32[]{:T(128)}, f32[16,256]{1,0:T(8,128)S(1)}, ...), condition=%wide.region_5.6_spmd.clone, body=%wide.region_2.5_spmd.clone.sunk | while | flops 565072640 | bytes 68425952 | solution.py:176
  295.1 145.4 %all-gather.30.cloned.1.call-done = bf16[1024,4096]{1,0:T(8,128)(2,1)} async-done(((bf16[256,4096]{1,0:T(8,128)(2,1)}), bf16[1024,4096]{1,0:T(8,128)(2,1)}) %all-gather.30.cloned.1.call-update) | async-done | bytes 8388624 | tf_op jit(solution)/shard_map/all_gather | solution.py:187
  448.8 141.3 %all-gather.32.cloned.1.call-done = bf16[4096,1024]{1,0:T(8,128)(2,1)} async-done(((bf16[1024,1024]{1,0:T(8,128)(2,1)}), bf16[4096,1024]{1,0:T(8,128)(2,1)}) %all-gather.32.cloned.1.call-update) | async-done | bytes 8388624 | tf_op jit(solution)/shard_map/all_gather | solution.py:189
  621.9 47.3 %while.37 = (s32[]{:T(128)}, f32[256,16,64]{0,2,1:T(8,128)}, bf16[1024,1024]{0,1:T(8,128)(2,1)}, bf16[1024,1024]{0,1:T(8,128)(2,1)}, bf16[1024,1024]{0,1:T(8,128...) while((s32[]{:T(128)}, f32[256,16,64]{0,2,1:T(8,128)}, ...), condition=%wide.region_19.20_spmd.clone, body=%wide.region_18.19_spmd.clone.sunk | while | flops 1365115648 | bytes 169269840 | solution.py:346
  672.6 38.9 %reduce-scatter.9.cloned.1.call-done = bf16[256,1024]{0,1:T(8,128)(2,1)} async-done(((bf16[1024,1024]{0,1:T(8,128)(2,1)}), bf16[256,1024]{0,1:T(8,128)(2,1)}) %reduce-scatter.9.cloned.1.call-update) | async-done | bytes 524304 | tf_op jit(solution)/shard_map/reduce_scatter | solution.py:349
  718.1 38.9 %reduce-scatter.11.cloned.1.call-done = bf16[256,1024]{0,1:T(8,128)(2,1)} async-done(((bf16[1024,1024]{0,1:T(8,128)(2,1)}), bf16[256,1024]{0,1:T(8,128)(2,1)}) %reduce-scatter.11.cloned.1.call-update) | async-done | bytes 524304 | tf_op jit(solution)/shard_map/reduce_scatter | solution.py:352
  777.4 25.1 %reduce-scatter.19.cloned.1.call-done = bf16[256,1024]{1,0:T(8,128)(2,1)} async-done(((bf16[1024,1024]{1,0:T(8,128)(2,1)}), bf16[256,1024]{1,0:T(8,128)(2,1)}) %reduce-scatter.19.cloned.1.call-update) | async-done | bytes 524304 | tf_op jit(solution)/shard_map/reduce_scatter | solution.py:387
  802.5 46.0 %reduce-scatter.13.cloned.1.call-done = bf16[256,1024]{1,0:T(8,128)(2,1)} async-done(((bf16[1024,1024]{1,0:T(8,128)(2,1)}), bf16[256,1024]{1,0:T(8,128)(2,1)}) %reduce-scatter.13.cloned.1.call-update) | async-done | bytes 524304 | tf_op jit(solution)/shard_map/reduce_scatter | solution.py:378
  848.5 45.5 %reduce-scatter.15.cloned.1.call-done = bf16[256,1024]{1,0:T(8,128)(2,1)} async-done(((bf16[1024,1024]{1,0:T(8,128)(2,1)}), bf16[256,1024]{1,0:T(8,128)(2,1)}) %reduce-scatter.15.cloned.1.call-update) | async-done | bytes 524304 | tf_op jit(solution)/shard_map/reduce_scatter | solution.py:381
  894.0 45.5 %reduce-scatter.17.cloned.1.call-done = bf16[256,1024]{1,0:T(8,128)(2,1)} async-done(((bf16[1024,1024]{1,0:T(8,128)(2,1)}), bf16[256,1024]{1,0:T(8,128)(2,1)}) %reduce-scatter.17.cloned.1.call-update) | async-done | bytes 524304 | tf_op jit(solution)/shard_map/reduce_scatter | solution.py:384
  939.5 146.0 %reduce-scatter.21.cloned.1.call-done = bf16[256,4096]{1,0:T(8,128)(2,1)} async-done(((bf16[1024,4096]{1,0:T(8,128)(2,1)}), bf16[256,4096]{1,0:T(8,128)(2,1)}) %reduce-scatter.21.cloned.1.call-update) | async-done | bytes 2097168 | tf_op jit(solution)/shard_map/reduce_scatter | solution.py:233
  1085.5 147.4 %reduce-scatter.23.cloned.1.call-done = bf16[1024,1024]{1,0:T(8,128)(2,1)} async-done(((bf16[4096,1024]{1,0:T(8,128)(2,1)}), bf16[1024,1024]{1,0:T(8,128)(2,1)}) %reduce-scatter.23.cloned.1.call-update) | async-done | bytes 2097168 | tf_op jit(solution)/shard_map/reduce_scatter | solution.py:239
  1239.7 18.5 %all-reduce.12 = (bf16[1024]{0:T(1024)(128)(2,1)S(1)}, bf16[1024]{0:T(1024)(128)(2,1)S(1)}, bf16[1024]{0:T(1024)(128)(2,1)S(1)}, bf16[1024]{0:T(1024)(128)(2,1)S...) all-reduce(bf16[1024]{0:T(1024)(128)(2,1)S(1)} %reduce_sum.286, ...), channel_id=5, replica_groups=mesh['rep'=8,'shard'=4] {'shard'}, use_global_device_ids=true, to_apply=%region_27.28.clone | all-reduce | flops 13312 | bytes 53248
  1258.8 13.2 all-reduce.10
  1279.1 64.2 %all-reduce.15.cloned.1.call-done = (bf16[256,1024]{1,0:T(8,128)(2,1)}, bf16[256,1024]{1,0:T(8,128)(2,1)}, bf16[256,1024]{1,0:T(8,128)(2,1)}, bf16[256,1024]{1,0...) async-done(((bf16[256,1024]{1,0:T(8,128)(2,1)}, bf16[256,1024]{1,0:T(8,128)(2,1)}, bf16[256,1024]{1,0:T(8,128)(2,1)}, bf16[256,1024]{1,0:T(8,128)(2,1)}, ...) | async-done | bytes 6291472 | tf_op jit(solution)/shard_map/psum | solution.py:423
  (340 shorter events, 258.5 us)
Async XLA Ops:
  7.2 97.4 %copy-start.13 = (bf16[256,1024]{1,0:T(8,128)(2,1)S(1)}, bf16[256,1024]{1,0:T(8,128)(2,1)}, u32[]{:S(2)}) copy-start(bf16[256,1024]{1,0:T(8,128)(2,1)} %param.22) | copy-start | bytes 1572868
  7.2 51.1 %all-gather.24.cloned.1.call-start = ((), (), s32[]{:S(2)}) async-start(), calls=%async_computation.11 | async-start | bytes 2621440 | tf_op jit(solution)/shard_map/all_gather | solution.py:99
  8.0 96.7 %all-gather.22.cloned.1.call-start = ((), (), s32[]{:S(2)}) async-start(), calls=%async_computation.10 | async-start | bytes 2621440 | tf_op jit(solution)/shard_map/all_gather | solution.py:97
  8.7 142.2 %all-gather.18.cloned.1.call-start = ((), (), s32[]{:S(2)}) async-start(), calls=%async_computation.8 | async-start | bytes 2621440 | tf_op jit(solution)/shard_map/all_gather | solution.py:98
  9.4 205.7 %all-gather.26.cloned.1.call-start = ((), (), s32[]{:S(2)}) async-start(), calls=%async_computation.12 | async-start | bytes 2621440 | tf_op jit(solution)/shard_map/all_gather | solution.py:144
  22.8 128.1 %copy-start.38 = (f32[4,1,256]{2,1,0:T(1,128)}, f32[4,1,256]{2,1,0:T(1,128)S(1)}, u32[]{:S(2)}) copy-start(f32[4,1,256]{2,1,0:T(1,128)S(1)} %convert_element_type.317) | copy-start | bytes 12292
  32.3 118.6 %copy-start.40 = (f32[256]{0:T(256)}, f32[256]{0:T(256)S(1)}, u32[]{:S(2)}) copy-start(f32[256]{0:T(256)S(1)} %broadcast_multiply_fusion.12) | copy-start | bytes 3076
  33.7 117.2 %copy-start.42 = (f32[256]{0:T(256)}, f32[256]{0:T(256)S(1)}, u32[]{:S(2)}) copy-start(f32[256]{0:T(256)S(1)} %add_rsqrt_fusion.3) | copy-start | bytes 3076
  61.7 183.3 %all-gather.20.cloned.1.call-start = ((), (), s32[]{:S(2)}) async-start(), calls=%async_computation.9 | async-start | bytes 2621440 | tf_op jit(solution)/shard_map/all_gather | solution.py:143
  80.0 75.8 %copy-start.35 = (f32[256,32]{0,1:T(8,128)}, f32[256,32]{0,1:T(8,128)S(1)}, u32[]{:S(2)}) copy-start(f32[256,32]{0,1:T(8,128)S(1)} %get-tuple-element.589) | copy-start | bytes 98308
  157.0 133.6 %all-gather.28.cloned.1.call-start = ((), (), s32[]{:S(2)}) async-start(), calls=%async_computation.13 | async-start | bytes 2621440 | tf_op jit(solution)/shard_map/all_gather | solution.py:100
  157.6 283.0 %all-gather.30.cloned.1.call-start = ((), (), s32[]{:S(2)}) async-start(), calls=%async_computation.14 | async-start | bytes 10485760 | tf_op jit(solution)/shard_map/all_gather | solution.py:187
  158.4 431.7 %all-gather.32.cloned.1.call-start = ((), (), s32[]{:S(2)}) async-start(), calls=%async_computation.15 | async-start | bytes 10485760 | tf_op jit(solution)/shard_map/all_gather | solution.py:189
  159.1 552.4 %reduce-scatter.9.cloned.1.call-start = ((), (), s32[]{:S(2)}) async-start(), calls=%async_computation.16 | async-start | bytes 2621440 | tf_op jit(solution)/shard_map/reduce_scatter | solution.py:349
  669.3 87.7 %reduce-scatter.11.cloned.1.call-start = ((), (), s32[]{:S(2)}) async-start(), calls=%async_computation.17 | async-start | bytes 2621440 | tf_op jit(solution)/shard_map/reduce_scatter | solution.py:352
  669.9 132.6 %reduce-scatter.19.cloned.1.call-start = ((), (), s32[]{:S(2)}) async-start(), calls=%async_computation.21 | async-start | bytes 2621440 | tf_op jit(solution)/shard_map/reduce_scatter | solution.py:387
  672.5 176.0 %reduce-scatter.13.cloned.1.call-start = ((), (), s32[]{:S(2)}) async-start(), calls=%async_computation.18 | async-start | bytes 2621440 | tf_op jit(solution)/shard_map/reduce_scatter | solution.py:378
  715.5 178.5 %reduce-scatter.15.cloned.1.call-start = ((), (), s32[]{:S(2)}) async-start(), calls=%async_computation.19 | async-start | bytes 2621440 | tf_op jit(solution)/shard_map/reduce_scatter | solution.py:381
  718.0 221.5 %reduce-scatter.17.cloned.1.call-start = ((), (), s32[]{:S(2)}) async-start(), calls=%async_computation.20 | async-start | bytes 2621440 | tf_op jit(solution)/shard_map/reduce_scatter | solution.py:384
  760.2 325.3 %reduce-scatter.21.cloned.1.call-start = ((), (), s32[]{:S(2)}) async-start(), calls=%async_computation.22 | async-start | bytes 10485760 | tf_op jit(solution)/shard_map/reduce_scatter | solution.py:233
  767.6 465.3 %reduce-scatter.23.cloned.1.call-start = ((), (), s32[]{:S(2)}) async-start(), calls=%async_computation.23 | async-start | bytes 10485760 | tf_op jit(solution)/shard_map/reduce_scatter | solution.py:239
  777.1 455.9 %copy-start.53 = (u32[32]{0:T(128)S(1)}, u32[32]{0:T(128)}, u32[]{:S(2)}) copy-start(u32[32]{0:T(128)} %constant.159) | copy-start | bytes 388
  777.1 457.9 %copy-start.29 = (bf16[256,1024]{0,1:T(8,128)(2,1)S(1)}, bf16[256,1024]{0,1:T(8,128)(2,1)}, u32[]{:S(2)}) copy-start(bf16[256,1024]{0,1:T(8,128)(2,1)} %reduce-scatter.11.cloned.1.call-done) | copy-start | bytes 1572868
  777.1 566.2 %all-reduce.15.cloned.1.call-start = ((), (), s32[]{:S(2)}) async-start(), calls=%async_computation.24 | async-start | bytes 12582912 | tf_op jit(solution)/shard_map/psum | solution.py:423
  (63 other events, 796.6 us)
Sparse Core Ops, SparseCore 0:
  9.6 48.6 all-gather.23
  59.9 44.6 all-gather.21
  106.2 44.6 all-gather.17
  152.9 44.8 all-gather.25
  199.8 45.1 all-gather.19
  246.4 44.1 all-gather.27
  292.2 148.3 all-gather.29
  442.1 147.8 all-gather.31
  669.4 42.0 reduce-scatter.8
  713.8 43.1 reduce-scatter.10
  759.3 43.1 reduce-scatter.18
  805.3 43.1 reduce-scatter.12
  850.8 43.1 reduce-scatter.14
  896.3 43.1 reduce-scatter.16
  941.7 143.7 reduce-scatter.20
  1087.7 145.1 reduce-scatter.22
  1236.8 106.4 all-reduce.14
where the time goes:
time: 1370 us; the launch traced here: 1360 us
  waiting for transfers between devices  1020 us (74%)
  blocking collectives  125 us (9%)
  matrix products  119 us (9%)
  other arithmetic  44.1 us (3%)
  local copies, waits for them, and re-layouts  40.1 us (3%)
  between operations  16.3 us (1%)
    reduce_scatter x1, waiting for transfers between devices, per_device(): lax.psum_scatter(grad_down.astype(jnp.bfloat16), 'shard', scatter_dimensi...  147 us
    reduce_scatter x1, waiting for transfers between devices, per_device(): lax.psum_scatter(grad_up.astype(jnp.bfloat16), 'shard', scatter_dimension...  146 us
    all_gather x1, waiting for transfers between devices, per_device(): lax.all_gather(feed_local[0], 'shard', axis=0, tiled=True)  145 us
    all_gather x1, waiting for transfers between devices, per_device(): lax.all_gather(feed_local[2], 'shard', axis=0, tiled=True)  141 us
    psum x1, waiting for transfers between devices, per_device(): lax.psum(g_query.astype(jnp.bfloat16), 'rep').astype(jnp.float32)  64.2 us
    reduce_scatter x1, waiting for transfers between devices, per_device(): lax.psum_scatter(grad_query_mat.astype(jnp.bfloat16), 'shard', scatter_di...  46 us
    reduce_scatter x1, waiting for transfers between devices, per_device(): lax.psum_scatter(grad_key_mat.astype(jnp.bfloat16), 'shard', scatter_dime...  45.5 us
    reduce_scatter x1, waiting for transfers between devices, per_device(): lax.psum_scatter(grad_value_mat.astype(jnp.bfloat16), 'shard', scatter_di...  45.5 us
  transfers between devices with their start and end apart: 17, of which 16 were waited for; matrix products, arithmetic and copies ran while one was open for 8% of the time, Pallas kernels for 0%

commit v1 on v0

--- a/solution.py
+++ b/solution.py
@@ -1,8 +1,12 @@
+import functools
 import math
 
 import jax
 import jax.numpy as jnp
+import numpy as np
 from jax import lax
+from jax.experimental import pallas as pl
+from jax.experimental.pallas import tpu as pltpu
 from jax.sharding import PartitionSpec as P
 
 HEADS = 16
@@ -45,7 +49,7 @@
     return jnp.sum(values.astype(jnp.float32), axis=0)
 
 
-def per_device(
+def general_device(
     layer_input,
     query_weight,
     query_bias,
@@ -459,9 +463,466 @@
     )
 
 
+def swap(values, bit):
+    count = lax.axis_size("rep")
+    return lax.ppermute(values, "rep", [(i, i ^ bit) for i in range(count)])
+
+
+def shift(values, step):
+    count = lax.axis_size("shard")
+    return lax.ppermute(values, "shard", [(i, (i + step) % count) for i in range(count)])
+
+
+def token_pairs(count):
+    pairs = []
+    for rep in range(count):
+        for z in range(4):
+            there = (rep & ~3) | ((z & 1) << 1) | (z >> 1)
+            pairs.append((rep * 4 + z, there * 4 + (rep & 3)))
+    return pairs
+
+
+def by_bit(bit, own, other):
+    return jnp.where(bit == 0, jnp.stack([own, other]), jnp.stack([other, own]))
+
+
+def pick(values, index, size, axis=0):
+    return lax.dynamic_slice_in_dim(values, index * size, size, axis)
+
+
+def gather_shards(piece, place):
+    out = jnp.zeros((4,) + piece.shape, piece.dtype)
+    out = lax.dynamic_update_index_in_dim(out, piece, place, 0)
+    for step in (1, 2, 3):
+        out = lax.dynamic_update_index_in_dim(out, shift(piece, step), (place + 4 - step) % 4, 0)
+    return out
+
+
+def rope_tables(tokens, head_dim):
+    half = head_dim // 2
+    freqs = 10000.0 ** (-np.arange(half, dtype=np.float64) / half)
+    angles = np.arange(tokens, dtype=np.float64)[:, None] * freqs[None, :]
+    cosines = np.tile(np.cos(angles), (1, 4)).astype(np.float32)
+    sines = np.tile(np.concatenate([-np.sin(angles), np.sin(angles)], 1), (1, 2)).astype(np.float32)
+    return jnp.asarray(cosines), jnp.asarray(sines)
+
+
+def turn(values, cosines, sines):
+    lane = lax.broadcasted_iota(jnp.int32, values.shape, 1)
+    swapped = jnp.where(
+        lane % 64 < 32, pltpu.roll(values, 96, 1), pltpu.roll(values, 32, 1)
+    )
+    return values * cosines + swapped * sines
+
+
+def nt(left, right):
+    return lax.dot_general(left, right, (((1,), (1,)), ((), ())), preferred_element_type=jnp.float32)
+
+
+def tn(left, right):
+    return lax.dot_general(left, right, (((0,), (0,)), ((), ())), preferred_element_type=jnp.float32)
+
+
+BLOCK = 256
+
+
+def head_lanes(shape, parity):
+    lane = lax.broadcasted_iota(jnp.int32, shape, 1)
+    return (lane // 64) == parity
+
+
+def attend_kernel(hidden, weights, shifts, cosines, sines, query, key, value, mixed, logs):
+    tokens = hidden.shape[0]
+    blocks = tokens // BLOCK
+    width = 256
+
+    def project(index, carry):
+        rows = pl.ds(pl.multiple_of(index * BLOCK, BLOCK), BLOCK)
+        raw = jnp.dot(hidden[rows, :], weights[...], preferred_element_type=jnp.float32) + shifts[...]
+        cos, sin = cosines[rows, :], sines[rows, :]
+        for tile in range(width // 128):
+            lanes = slice(tile * 128, tile * 128 + 128)
+            query[rows, lanes] = (
+                turn(raw[:, lanes], cos, sin).astype(jnp.bfloat16) * jnp.bfloat16(0.125)
+            )
+            key[rows, lanes] = turn(raw[:, width:][:, lanes], cos, sin).astype(jnp.bfloat16)
+        value[rows, :] = raw[:, 2 * width :].astype(jnp.bfloat16)
+        return carry
+
+    lax.fori_loop(0, blocks, project, 0)
+    causal = lax.broadcasted_iota(jnp.int32, (BLOCK, BLOCK), 0) >= lax.broadcasted_iota(
+        jnp.int32, (BLOCK, BLOCK), 1
+    )
+    logs[...] = jnp.zeros_like(logs)
+
+    def pair_step(pair, carry):
+        lanes = pl.ds(pl.multiple_of(pair * 128, 128), 128)
+        lane = lax.broadcasted_iota(jnp.int32, (BLOCK, 128), 1)
+        for block in range(blocks):
+            rows = slice(block * BLOCK, block * BLOCK + BLOCK)
+            seen = (block + 1) * BLOCK
+            queries = query[rows, lanes]
+            keys, values = key[:seen, lanes], value[:seen, lanes]
+            outs = []
+            log_rows = logs[rows, :]
+            for parity in range(2):
+                masked = jnp.where(head_lanes(queries.shape, parity), queries, jnp.bfloat16(0))
+                scores = nt(masked, keys)
+                last = jnp.where(causal, scores[:, seen - BLOCK :], -1e30)
+                if block:
+                    scores = jnp.concatenate([scores[:, : seen - BLOCK], last], 1)
+                else:
+                    scores = last
+                best = jnp.max(scores, axis=1, keepdims=True)
+                exps = jnp.exp(scores - best)
+                total = jnp.sum(exps, axis=1, keepdims=True)
+                out = jnp.dot(exps.astype(jnp.bfloat16), values, preferred_element_type=jnp.float32)
+                outs.append(out / total)
+                log_rows = jnp.where(lane == pair * 2 + parity, best + jnp.log(total), log_rows)
+            mixed[rows, lanes] = jnp.where(lane < 64, outs[0], outs[1]).astype(jnp.bfloat16)
+            logs[rows, :] = log_rows
+        return carry
+
+    lax.fori_loop(0, 2, pair_step, 0)
+
+
+def attend(hidden, weights, shifts, cosines, sines):
+    tokens = hidden.shape[0]
+    shaped = lambda width, kind: jax.ShapeDtypeStruct((tokens, width), kind)
+    return pl.pallas_call(
+        attend_kernel,
+        out_shape=(
+            shaped(256, jnp.bfloat16),
+            shaped(256, jnp.bfloat16),
+            shaped(256, jnp.bfloat16),
+            shaped(256, jnp.bfloat16),
+            shaped(128, jnp.float32),
+        ),
+        in_specs=[pl.BlockSpec(memory_space=pltpu.VMEM)] * 5,
+        out_specs=[pl.BlockSpec(memory_space=pltpu.VMEM)] * 5,
+        compiler_params=pltpu.CompilerParams(vmem_limit_bytes=48 << 20),
+        cost_estimate=pl.CostEstimate(
+            flops=2 * tokens * 1024 * 768 + 16 * tokens * tokens * 64,
+            bytes_accessed=8 << 20,
+            transcendentals=4 * tokens * tokens,
+        ),
+        name="attend",
+    )(hidden, weights, shifts, cosines, sines)
+
+
+def attend_back_kernel(
+    upstream, out_rows, query, key, value, mixed, logs, cosines, sines, grads, d_out, d_key, d_value, d_query
+):
+    tokens = upstream.shape[0]
+    blocks = tokens // BLOCK
+    width = 256
+
+    def project(index, carry):
+        rows = pl.ds(pl.multiple_of(index * BLOCK, BLOCK), BLOCK)
+        d_out[rows, :] = nt(upstream[rows, :], out_rows[...]).astype(jnp.bfloat16)
+        return carry
+
+    lax.fori_loop(0, blocks, project, 0)
+    d_key[...] = jnp.zeros_like(d_key)
+    d_value[...] = jnp.zeros_like(d_value)
+    d_query[...] = jnp.zeros_like(d_query)
+    causal = lax.broadcasted_iota(jnp.int32, (BLOCK, BLOCK), 0) >= lax.broadcasted_iota(
+        jnp.int32, (BLOCK, BLOCK), 1
+    )
+
+    def pair_step(pair, carry):
+        lanes = pl.ds(pl.multiple_of(pair * 128, 128), 128)
+        for block in range(blocks):
+            rows = slice(block * BLOCK, block * BLOCK + BLOCK)
+            seen = (block + 1) * BLOCK
+            queries, d_outs = query[rows, lanes], d_out[rows, lanes]
+            keys, values = key[:seen, lanes], value[:seen, lanes]
+            products = d_outs.astype(jnp.float32) * mixed[rows, lanes].astype(jnp.float32)
+            log_rows = logs[rows, :]
+            lane = lax.broadcasted_iota(jnp.int32, (BLOCK, 128), 1)
+            for parity in range(2):
+                mine = head_lanes((BLOCK, 128), parity)
+                masked_q = jnp.where(mine, queries, jnp.bfloat16(0))
+                masked_d = jnp.where(mine, d_outs, jnp.bfloat16(0))
+                log = jnp.sum(jnp.where(lane == pair * 2 + parity, log_rows, 0.0), 1, keepdims=True)
+                delta = jnp.sum(jnp.where(mine, products, 0.0), 1, keepdims=True)
+                scores = nt(masked_q, keys)
+                probs = jnp.exp(scores - log)
+                last = jnp.where(causal, probs[:, seen - BLOCK :], 0.0)
+                if block:
+                    probs = jnp.concatenate([probs[:, : seen - BLOCK], last], 1)
+                else:
+                    probs = last
+                d_probs = nt(masked_d, values)
+                d_scores = (probs * (d_probs - delta)).astype(jnp.bfloat16)
+                probs = probs.astype(jnp.bfloat16)
+                d_query[rows, lanes] += jnp.where(
+                    mine, jnp.dot(d_scores, keys, preferred_element_type=jnp.float32), 0.0
+                )
+                d_value[:seen, lanes] += tn(probs, masked_d)
+                d_key[:seen, lanes] += tn(d_scores, masked_q)
+        return carry
+
+    lax.fori_loop(0, 2, pair_step, 0)
+
+    def finish(index, carry):
+        rows = pl.ds(pl.multiple_of(index * BLOCK, BLOCK), BLOCK)
+        cos, sin = cosines[rows, :], -sines[rows, :]
+        for tile in range(width // 128):
+            lanes = slice(tile * 128, tile * 128 + 128)
+            at = tile * 128
+            grads[rows, at : at + 128] = turn(d_query[rows, lanes] * 0.125, cos, sin).astype(jnp.bfloat16)
+            at += width
+            grads[rows, at : at + 128] = turn(d_key[rows, lanes], cos, sin).astype(jnp.bfloat16)
+        grads[rows, 2 * width :] = d_value[rows, :].astype(jnp.bfloat16)
+        return carry
+
+    lax.fori_loop(0, blocks, finish, 0)
+
+
+def attend_back(upstream, out_rows, query, key, value, mixed, logs, cosines, sines):
+    tokens = upstream.shape[0]
+    return pl.pallas_call(
+        attend_back_kernel,
+        out_shape=jax.ShapeDtypeStruct((tokens, 768), jnp.bfloat16),
+        in_specs=[pl.BlockSpec(memory_space=pltpu.VMEM)] * 9,
+        out_specs=pl.BlockSpec(memory_space=pltpu.VMEM),
+        scratch_shapes=[
+            pltpu.VMEM((tokens, 256), jnp.bfloat16),
+            pltpu.VMEM((tokens, 256), jnp.float32),
+            pltpu.VMEM((tokens, 256), jnp.float32),
+            pltpu.VMEM((tokens, 256), jnp.float32),
+        ],
+        compiler_params=pltpu.CompilerParams(vmem_limit_bytes=48 << 20),
+        cost_estimate=pl.CostEstimate(
+            flops=2 * tokens * 1024 * 256 + 40 * tokens * tokens * 64,
+            bytes_accessed=8 << 20,
+            transcendentals=4 * tokens * tokens,
+        ),
+        name="attend_back",
+    )(upstream, out_rows, query, key, value, mixed, logs, cosines, sines)
+
+
+def fast_device(
+    layer_input,
+    query_weight,
+    query_bias,
+    key_weight,
+    key_bias,
+    value_weight,
+    value_bias,
+    output_weight,
+    output_bias,
+    up_weight,
+    up_bias,
+    down_weight,
+    down_bias,
+    attention_gain_in,
+    attention_gain_out,
+    feedforward_gain_in,
+    feedforward_gain_out,
+    layer_cotangent,
+):
+    f32, bf16 = jnp.float32, jnp.bfloat16
+    replicas = lax.axis_size("rep")
+    rows, width = layer_input.shape
+    tokens = rows * 4
+    rep, place = lax.axis_index("rep"), lax.axis_index("shard")
+    core, x_bit, y_bit = rep & 1, (rep >> 1) & 1, rep >> 2
+    quarter = rep & 3
+    wide = up_weight.shape[1]
+    local = wide // 4
+    block = local // 4
+    pairs = token_pairs(replicas)
+    back_pairs = [(there, here) for here, there in pairs]
+    both = ("rep", "shard")
+
+    own_rows = lax.ppermute(layer_input, both, pairs)
+
+    def head_columns(weight):
+        return weight.reshape(rows, 4, 4, 64)[:, :, quarter, :].reshape(rows, 256)
+
+    qkv_piece = jnp.concatenate(
+        [head_columns(query_weight), head_columns(key_weight), head_columns(value_weight)], 1
+    )
+    small_piece = jnp.concatenate(
+        [
+            query_bias,
+            key_bias,
+            value_bias,
+            output_bias,
+            down_bias,
+            attention_gain_in,
+            attention_gain_out,
+            feedforward_gain_in,
+            feedforward_gain_out,
+            up_bias,
+        ]
+    )
+    small_piece = small_piece.reshape(-1, 128)
+    small = gather_shards(small_piece, place).reshape(4, -1).astype(f32)
+    per = width // 4
+
+    def whole(index):
+        return small[:, index * per : (index + 1) * per].reshape(width)
+
+    def local_heads(index):
+        return small[:, index * per : (index + 1) * per].reshape(4, 4, 64)[:, quarter, :].reshape(256)
+
+    out_shift, down_shift = whole(3), whole(4)
+    gain_in_a, gain_out_a, gain_in_f, gain_out_f = whole(5), whole(6), whole(7), whole(8)
+    up_shift = small[:, 9 * per :].reshape(4, 4, block)[:, quarter, :].reshape(local)
+    qkv_shift = jnp.concatenate([local_heads(0), local_heads(1), local_heads(2)]).reshape(1, 768)
+
+    qkv = gather_shards(qkv_piece, place).reshape(width, 768)
+    out_rows = gather_shards(pick(output_weight, quarter, 64), place).reshape(256, width)
+    up_piece = jnp.concatenate([pick(up_weight, 4 * i + quarter, block, 1) for i in range(4)], 1)
+    up_mat = gather_shards(up_piece, place).reshape(width, local)
+    down_mat = gather_shards(pick(down_weight, quarter, block), place).reshape(local, width)
+
+    def gather_group(values):
+        mine = by_bit(x_bit, values, swap(values, 2)).reshape(2 * rows, width)
+        return by_bit(core, mine, swap(mine, 1)).reshape(tokens, width)
+
+    def scatter_group(partial):
+        there = pick(partial, 1 - core, 2 * rows).astype(bf16)
+        partial = pick(partial, core, 2 * rows) + swap(there, 1).astype(f32)
+        there = pick(partial, 1 - x_bit, rows).astype(bf16)
+        return pick(partial, x_bit, rows) + swap(there, 2).astype(f32)
+
+    residual_in = own_rows.astype(f32)
+    normed_a, inverse_a = normalize(residual_in)
+    hidden_a = gather_group((normed_a * gain_in_a).astype(bf16))
+    cosines, sines = rope_tables(tokens, 64)
+    query, key, value, mixed, logs = attend(hidden_a, qkv, qkv_shift, cosines, sines)
+    branch_a = scatter_group(jnp.dot(mixed, out_rows, preferred_element_type=f32)) + out_shift
+    normed_o, inverse_o = normalize(branch_a)
+    middle = residual_in + normed_o * gain_out_a
+    normed_f, inverse_f = normalize(middle)
+    hidden_f = gather_group((normed_f * gain_in_f).astype(bf16))
+    pre_act = jnp.dot(hidden_f, up_mat, preferred_element_type=f32) + up_shift
+    activated = jax.nn.gelu(pre_act).astype(bf16)
+    branch_f = scatter_group(jnp.dot(activated, down_mat, preferred_element_type=f32)) + down_shift
+    normed_d, inverse_d = normalize(branch_f)
+    layer_output = (middle + normed_d * gain_out_f).astype(bf16)
+    layer_output = lax.ppermute(layer_output, both, back_pairs)
+
+    upstream = lax.ppermute(layer_cotangent, both, pairs).astype(f32)
+    grad_gain_out_f = jnp.sum(upstream * normed_d, axis=0)
+    d_branch_f = norm_back(normed_d, inverse_d, upstream * gain_out_f).astype(bf16)
+    grad_down_shift = col_sum(d_branch_f)
+    d_branch_f = gather_group(d_branch_f)
+    grad_down = tn(activated, d_branch_f).astype(bf16)
+    d_activated = nt(d_branch_f, down_mat)
+    gelu_out, gelu_pull = jax.vjp(jax.nn.gelu, pre_act)
+    d_pre = gelu_pull(d_activated)[0].astype(bf16)
+    grad_up = tn(hidden_f, d_pre).astype(bf16)
+    grad_up_shift = col_sum(d_pre)
+    d_hidden_f = scatter_group(nt(d_pre, up_mat))
+    grad_gain_in_f = jnp.sum(d_hidden_f * normed_f, axis=0)
+    d_middle = upstream + norm_back(normed_f, inverse_f, d_hidden_f * gain_in_f)
+    grad_gain_out_a = jnp.sum(d_middle * normed_o, axis=0)
+    d_branch_a = norm_back(normed_o, inverse_o, d_middle * gain_out_a).astype(bf16)
+    grad_out_shift = col_sum(d_branch_a)
+    d_branch_a = gather_group(d_branch_a)
+    grad_out = tn(mixed, d_branch_a).astype(bf16)
+    d_qkv = attend_back(
+        d_branch_a, out_rows, query, key, value, mixed, logs, cosines, sines
+    )
+    grad_qkv = tn(hidden_a, d_qkv).astype(bf16)
+    grad_qkv_shift = col_sum(d_qkv)
+    d_hidden_a = scatter_group(nt(d_qkv, qkv))
+    grad_gain_in_a = jnp.sum(d_hidden_a * normed_a, axis=0)
+    input_gradient = d_middle + norm_back(normed_a, inverse_a, d_hidden_a * gain_in_a)
+    input_gradient = lax.ppermute(input_gradient.astype(bf16), both, back_pairs).astype(f32)
+
+    def reduce_grad(grad):
+        size = grad.shape[1]
+        if replicas == 8:
+            half = size // 2
+            there = swap(pick(grad, 1 - y_bit, half, 1), 4)
+            grad = (pick(grad, y_bit, half, 1).astype(f32) + there.astype(f32)).astype(bf16)
+        total = lax.dynamic_index_in_dim(grad, place, 0, False).astype(f32)
+        for step in (1, 2, 3):
+            sent = lax.dynamic_index_in_dim(grad, (place + step) % 4, 0, False)
+            total = total + shift(sent, step).astype(f32)
+        total = total.astype(bf16)
+        total = by_bit(x_bit, total, swap(total, 2))
+        if replicas == 8:
+            total = by_bit(y_bit, total, swap(total, 4))
+        else:
+            total = total[None]
+        return by_bit(core, total, swap(total, 1))
+
+    def by_rows(total):
+        return total.transpose(2, 0, 1, 3, 4).reshape(-1, total.shape[-1]).astype(f32)
+
+    g_down = by_rows(reduce_grad(grad_down.reshape(4, block, width)))
+    g_up = reduce_grad(grad_up.reshape(4, rows, local))
+    g_up = (
+        g_up.reshape(2, -1, 2, g_up.shape[3], 4, block)
+        .transpose(1, 3, 4, 2, 0, 5)
+        .reshape(rows, wide)
+        .astype(f32)
+    )
+    g_out = by_rows(reduce_grad(grad_out.reshape(4, 64, width)))
+    g_qkv = reduce_grad(grad_qkv.reshape(4, rows, 768))
+    g_qkv = (
+        g_qkv.reshape(2, -1, 2, g_qkv.shape[3], 3, 4, 64)
+        .transpose(4, 1, 3, 5, 2, 0, 6)
+        .reshape(3, rows, width)
+        .astype(f32)
+    )
+
+    def spread(values, size):
+        out = jnp.zeros((4, 4, size), f32)
+        return lax.dynamic_update_slice(out, values.reshape(4, 1, size), (0, quarter, 0)).reshape(4, -1)
+
+    vectors = [spread(grad_qkv_shift[i * 256 : (i + 1) * 256], 64) for i in range(3)]
+    for item in (
+        grad_out_shift,
+        grad_down_shift,
+        grad_gain_in_a,
+        grad_gain_out_a,
+        grad_gain_in_f,
+        grad_gain_out_f,
+    ):
+        vectors.append(item.reshape(4, per))
+    vectors.append(spread(grad_up_shift, block))
+    vector = jnp.concatenate(vectors, 1)
+    vector = lax.psum(vector, both)
+    vector = lax.dynamic_index_in_dim(vector, place, 0, False)
+
+    def own(index):
+        return vector[index * per : (index + 1) * per]
+
+    return (
+        layer_output,
+        input_gradient,
+        g_qkv[0],
+        own(0),
+        g_qkv[1],
+        own(1),
+        g_qkv[2],
+        own(2),
+        g_out,
+        own(3),
+        g_up,
+        vector[9 * per :],
+        g_down,
+        own(4),
+        own(5),
+        own(6),
+        own(7),
+        own(8),
+    )
+
+
 def solution(mesh):
+    replicas, shards = mesh.shape["rep"], mesh.shape["shard"]
+    fits = shards == 4 and replicas in (4, 8) and HEADS % 16 == 0
     return jax.shard_map(
-        per_device,
+        fast_device if fits else general_device,
         mesh=mesh,
         in_specs=(
             P(("rep", "shard"), None),

time: 1370 us -> 658 us (0.48)
  waiting for transfers between devices: 1020 us -> 170 us
  starting transfers between devices: 1.06 us -> 172 us
  local copies, waits for them, and re-layouts: 40.1 us -> 122 us
  blocking collectives: 125 us -> 43.5 us
  matrix products: 119 us -> 38.5 us
  other arithmetic: 44.1 us -> 73.2 us
  Pallas kernels: 0 us -> 24.2 us
  between operations: 16.3 us -> 2.51 us
    reduce_scatter x8 -> x0, waiting for transfers between devices: 533 us -> none  [the longest x1 147 us: per_device(): lax.psum_scatter(grad_down.astype(jnp.bfloat16), 'shard', scatter_dimensi...]
    all_gather x8 -> x0, waiting for transfers between devices: 414 us -> none  [the longest x1 145 us: per_device(): lax.all_gather(feed_local[0], 'shard', axis=0, tiled=True)]
    ppermute x0 -> x63, starting transfers between devices: none -> 172 us  [the longest x27 105 us: shift(): lax.ppermute(values, 'shard', [(i, (i + step) % count) for i in range(cou...]
    ppermute x0 -> x63, waiting for transfers between devices: none -> 170 us  [the longest x27 94.8 us: shift(): lax.ppermute(values, 'shard', [(i, (i + step) % count) for i in range(cou...]
    all_gather x10 -> x0, blocking collectives: 93.4 us -> none  [the longest x1 12.6 us: per_device(): lax.all_gather(attention_local[8], 'shard', axis=0, tiled=True)]
    dot_general x32 -> x10, matrix products: 119 us -> 38.5 us  [the longest x3 14.2 us: nt(): lax.dot_general(left, right, (((1,), (1,)), ((), ())), preferred_element_...]
    psum x1 -> x0, waiting for transfers between devices: 64.2 us -> none  [per_device(): lax.psum(g_query.astype(jnp.bfloat16), 'rep').astype(jnp.float32)]
    unnamed x109 -> x149, local copies, waits for them, and re-layouts: 9.73 us -> 55.6 us
  transfers between devices with their start and end apart: 17 -> 63, of which waited for: 16 -> 25; matrix products, arithmetic and copies ran while one was open for 8% -> 24% of each run, Pallas kernels for 0% -> 2%
where the time goes in v1:
time: 658 us; the launch traced here: 647 us
  starting transfers between devices  172 us (26%)
  waiting for transfers between devices  170 us (26%)
  local copies, waits for them, and re-layouts  122 us (19%)
  other arithmetic  73.2 us (11%)
  blocking collectives  43.5 us (7%)
  matrix products  38.5 us (6%)
  Pallas kernels  24.2 us (4%)
    ppermute x27, starting transfers between devices, shift(): lax.ppermute(values, 'shard', [(i, (i + step) % count) for i in range(cou...  105 us
    ppermute x27, waiting for transfers between devices, shift(): lax.ppermute(values, 'shard', [(i, (i + step) % count) for i in range(cou...  94.8 us
    ppermute x32, waiting for transfers between devices, swap(): return lax.ppermute(values, 'rep', [(i, i ^ bit) for i in range(count)])  75.7 us
    ppermute x32, starting transfers between devices, swap(): return lax.ppermute(values, 'rep', [(i, i ^ bit) for i in range(count)])  58.7 us
    unnamed x149, local copies, waits for them, and re-layouts  55.6 us
    psum x1, blocking collectives, fast_device(): vector = lax.psum(vector, both)  43.5 us
    select_n x25, other arithmetic, by_bit(): return jnp.where(bit == 0, jnp.stack([own, other]), jnp.stack([other, own]))  32.1 us
    dot_general x3, matrix products, nt(): lax.dot_general(left, right, (((1,), (1,)), ((), ())), preferred_element_...  14.2 us
  transfers between devices with their start and end apart: 63, of which 25 were waited for; matrix products, arithmetic and copies ran while one was open for 24% of the time, Pallas kernels for 2%

profile of v1, /device:TPU:0, one launch (start us, length us, event | category | flops | bytes accessed | tf_op | source)
XLA Modules:
  0.0 646.8 jit_solution(14436911059451396046)
XLA Ops:
  27.7 32.3 %collective-permute-start.4 = (bf16[256,1024]{1,0:T(8,128)(2,1)}, bf16[256,1024]{1,0:T(8,128)(2,1)}, u32[]{:S(2)}, u32[]{:S(2)}) collective-permute-start(bf16[256,1024]{1,0:T(8,128)(2,1)} %fusion.16), channel_id=1, source_target_pairs={{0,8},{4,12},{8,0},{12,4},{16,24},{20,28},{24,16},{28,20},{1,9},{5... | collective-permute-start | bytes 1572872 | tf_op jit(solution)/shard_map/ppermute | solution.py:468
  61.6 23.0 %collective-permute-start.10 = (bf16[64,1024]{1,0:T(8,128)(2,1)}, bf16[64,1024]{1,0:T(8,128)(2,1)}, u32[]{:S(2)}, u32[]{:S(2)}) collective-permute-start(bf16[64,1024]{1,0:T(8,128)(2,1)} %get-tuple-element.110), channel_id=1, source_target_pairs={{0,2},{1,3},{2,0},{3,1},{4,6},{5,7},{6,4},{7,5},{8,10},{9,11},{10,... | collective-permute-start | bytes 393224 | tf_op jit(solution)/shard_map/ppermute | solution.py:473
  85.9 7.6 %collective-permute-start.9 = (bf16[64,1024]{1,0:T(8,128)(2,1)}, bf16[64,1024]{1,0:T(8,128)(2,1)S(1)}, u32[]{:S(2)}, u32[]{:S(2)}) collective-permute-start(bf16[64,1024]{1,0:T(8,128)(2,1)} %get-tuple-element.110), channel_id=1, source_target_pairs={{0,1},{1,2},{2,3},{3,0},{4,5},{5,6},{6,7},{7,4},{8,9},{9,10},{10,1... | collective-permute-start | bytes 393224 | tf_op jit(solution)/shard_map/ppermute | solution.py:473
  97.4 5.7 collective-permute-done.11
  114.8 11.1 %attend.1 = (bf16[1024,256]{1,0:T(8,128)(2,1)S(1)}, bf16[1024,256]{1,0:T(8,128)(2,1)S(1)}, bf16[1024,256]{1,0:T(8,128)(2,1)S(1)}, bf16[1024,256]{1,0:T(8,128)(2,1)S(1)}, f32[1024,128]{1,0:T(8,128)S(1)}) custom-call(bf16[1024,1024]{1,0:T(8,128)(2,1)} %bitcast.247, bf16[1024,768]{1,0:T(8,128)(2,1)S(1)} %bitcast.220, f32[1,768]{1,0:T(1,128)S(1)} %reshape.1191.shifts, ...), custom_call_target="tpu_custom_call" | custom-call | flops 2684354560 | bytes 8388608 | tf_op jit(solution)/shard_map/attend/pallas_call | solution.py:592
  155.8 33.7 %collective-permute-done.19 = bf16[256,1024]{1,0:T(8,128)(2,1)} collective-permute-done((bf16[256,1024]{1,0:T(8,128)(2,1)}, bf16[256,1024]{1,0:T(8,128)(2,1)}, u32[]{:S(2)}, u32[]{:S(2)}) %collective-permute-start.19) | collective-permute-done | bytes 524320 | tf_op jit(solution)/shard_map/ppermute | solution.py:473
  191.5 34.7 %collective-permute-start.18 = (bf16[256,1024]{1,0:T(8,128)(2,1)}, bf16[256,1024]{1,0:T(8,128)(2,1)S(1)}, u32[]{:S(2)}, u32[]{:S(2)}) collective-permute-start(bf16[256,1024]{1,0:T(8,128)(2,1)} %pad_maximum_fusion), channel_id=1, source_target_pairs={{0,3},{1,0},{2,1},{3,2},{4,7},{5,4},{6,5},{7,6},{8,11},{9,8},{10,9... | collective-permute-start | bytes 1572872 | tf_op jit(solution)/shard_map/ppermute | solution.py:473
  228.3 5.3 collective-permute-done.21
  238.3 5.4 collective-permute-done.18
  249.6 5.9 fusion.46
  259.9 22.1 %collective-permute-done.23 = bf16[256,1024]{1,0:T(8,128)(2,1)S(1)} collective-permute-done((bf16[256,1024]{1,0:T(8,128)(2,1)S(1)}, bf16[256,1024]{1,0:T(8,128)(2,1)S(1)}, u32[]{:S(2)}, u32[]{:S(2)}) %collective-permute-start.23) | collective-permute-done | bytes 524320 | tf_op jit(solution)/shard_map/ppermute | solution.py:468
  286.8 10.1 %collective-permute-done.26 = bf16[256,1024]{1,0:T(8,128)(2,1)S(1)} collective-permute-done((bf16[256,1024]{1,0:T(8,128)(2,1)S(1)}, bf16[256,1024]{1,0:T(8,128)(2,1)S(1)}, u32[]{:S(2)}, u32[]{:S(2)}) %collective-permute-start.26) | collective-permute-done | bytes 524320 | tf_op jit(solution)/shard_map/ppermute | solution.py:468
  306.6 7.0 %convert_reduce_fusion = (f32[1024]{0:T(1024)S(1)}, bf16[1024,1024]{1,0:T(8,128)(2,1)S(1)}) fusion(f32[1024,1024]{1,0:T(8,128)S(1)} %copy-done.51, f32[1024]{0:T(1024)S(1)} %bitcast.306, bf16[1024,1024]{1,0:T(8,128)(2,1)S(1)} %bitcast.251, bf16[1024,1024]{1,0:T(8,128)(2,1)} %bitcast.43), kind=kOutput, calls=%fused_computation.11 | convolution fusion | flops 2171599872 | bytes 10493952 | tf_op jit(solution)/shard_map/dot_general | solution.py:519
  336.5 5.4 collective-permute-start.24
  358.4 15.8 %collective-permute-done.49 = bf16[4,128,1024]{1,2,0:T(8,128)(2,1)} collective-permute-done((bf16[4,128,1024]{1,2,0:T(8,128)(2,1)}, bf16[4,128,1024]{1,2,0:T(8,128)(2,1)}, u32[]{:S(2)}, u32[]{:S(2)}) %collective-permute-start.49) | collective-permute-done | bytes 1048608 | tf_op jit(solution)/shard_map/ppermute | solution.py:468
  383.9 13.3 %collective-permute-done.58 = bf16[128,1024]{0,1:T(8,128)(2,1)S(1)} collective-permute-done((bf16[128,1024]{0,1:T(8,128)(2,1)S(1)}, bf16[128,1024]{0,1:T(8,128)(2,1)S(1)}, u32[]{:S(2)}, u32[]{:S(2)}) %collective-permute-start.58) | collective-permute-done | bytes 262176 | tf_op jit(solution)/shard_map/ppermute | solution.py:473
  402.1 10.5 %collective-permute-done.51 = bf16[128,1024]{0,1:T(8,128)(2,1)S(1)} collective-permute-done((bf16[128,1024]{0,1:T(8,128)(2,1)S(1)}, bf16[128,1024]{0,1:T(8,128)(2,1)S(1)}, u32[]{:S(2)}, u32[]{:S(2)}) %collective-permute-start.51) | collective-permute-done | bytes 262176 | tf_op jit(solution)/shard_map/ppermute | solution.py:473
  451.4 13.0 %attend_back.1 = bf16[1024,768]{1,0:T(8,128)(2,1)S(1)} custom-call(bf16[1024,1024]{1,0:T(8,128)(2,1)} %bitcast.222, bf16[256,1024]{1,0:T(8,128)(2,1)S(1)} %bitcast.219, bf16[1024,256]{1,0:T(8,128)(2,1)S(1)} %copy-done.5, bf16[1024,256]{1,0:T(8,128)(2,1)S(1)} %copy-done.7, bf16[1024,256]{1,0:T(8,128)(2,1)S(1)} %copy-done.9, ...), custom_call_target="tpu_custom_call" | custom-call | flops 3221225472 | bytes 8388608 | tf_op jit(solution)/shard_map/attend_back/pallas_call | solution.py:685
  489.4 7.5 %copy.127 = f32[2,128,4,2,2,256]{5,4,3,2,1,0:T(2,128)} copy(f32[2,128,4,2,2,256]{5,1,2,3,0,4:T(8,128)} %convert_bitcast_fusion.1) | data formatting | bytes 8388608 | tf_op jit(solution)/shard_map/convert_element_type | solution.py:866
  496.9 6.4 reshape.1219
  503.4 5.4 copy.130
  533.0 5.5 collective-permute-done.36
  538.5 9.3 %collective-permute-done.37 = bf16[128,768]{0,1:T(8,128)(2,1)S(1)} collective-permute-done((bf16[128,768]{0,1:T(8,128)(2,1)S(1)}, bf16[128,768]{0,1:T(8,128)(2,1)S(1)}, u32[]{:S(2)}, u32[]{:S(2)}) %collective-permute-start.37) | collective-permute-done | bytes 196640 | tf_op jit(solution)/shard_map/ppermute | solution.py:473
  577.6 43.5 %psum.7 = f32[4,3328]{1,0:T(4,128)S(1)} all-reduce(f32[4,3328]{1,0:T(4,128)} %constant_dynamic-update-slice_fusion), channel_id=1, replica_groups=mesh['rep'=8,'shard'=4] {'rep','shard'}, use_global_device_ids=true, to_apply=%region_24.25 | all-reduce | flops 13312 | bytes 106496 | tf_op jit(solution)/shard_map/psum | solution.py:893
  (443 shorter events, 304.8 us)
Async XLA Ops:
  18.8 84.3 %collective-permute-start.7 = (bf16[256,768]{0,1:T(8,128)(2,1)}, bf16[256,768]{0,1:T(8,128)(2,1)}, u32[]{:S(2)}, u32[]{:S(2)}) collective-permute-start(bf16[256,768]{0,1:T(8,128)(2,1)} %get-tuple-element.134), channel_id=1, source_target_pairs={{0,2},{1,3},{2,0},{3,1},{4,6},{5,7},{6,4},{7,5},{8,10},{9,11},{10,... | collective-permute-start | bytes 1179656 | tf_op jit(solution)/shard_map/ppermute | solution.py:473
  20.7 83.6 %collective-permute-start.6 = (bf16[256,768]{0,1:T(8,128)(2,1)}, bf16[256,768]{0,1:T(8,128)(2,1)}, u32[]{:S(2)}, u32[]{:S(2)}) collective-permute-start(bf16[256,768]{0,1:T(8,128)(2,1)} %get-tuple-element.134), channel_id=1, source_target_pairs={{0,1},{1,2},{2,3},{3,0},{4,5},{5,6},{6,7},{7,4},{8,9},{9,10},{10,1... | collective-permute-start | bytes 1179656 | tf_op jit(solution)/shard_map/ppermute | solution.py:473
  22.3 84.0 %collective-permute-start.8 = (bf16[256,768]{0,1:T(8,128)(2,1)}, bf16[256,768]{0,1:T(8,128)(2,1)}, u32[]{:S(2)}, u32[]{:S(2)}) collective-permute-start(bf16[256,768]{0,1:T(8,128)(2,1)} %get-tuple-element.134), channel_id=1, source_target_pairs={{0,3},{1,0},{2,1},{3,2},{4,7},{5,4},{6,5},{7,6},{8,11},{9,8},{10,9... | collective-permute-start | bytes 1179656 | tf_op jit(solution)/shard_map/ppermute | solution.py:473
  27.7 58.1 %collective-permute-start.4 = (bf16[256,1024]{1,0:T(8,128)(2,1)}, bf16[256,1024]{1,0:T(8,128)(2,1)}, u32[]{:S(2)}, u32[]{:S(2)}) collective-permute-start(bf16[256,1024]{1,0:T(8,128)(2,1)} %fusion.16), channel_id=1, source_target_pairs={{0,8},{4,12},{8,0},{12,4},{16,24},{20,28},{24,16},{28,20},{1,9},{5... | collective-permute-start | bytes 1572872 | tf_op jit(solution)/shard_map/ppermute | solution.py:468
  61.6 34.7 %collective-permute-start.10 = (bf16[64,1024]{1,0:T(8,128)(2,1)}, bf16[64,1024]{1,0:T(8,128)(2,1)}, u32[]{:S(2)}, u32[]{:S(2)}) collective-permute-start(bf16[64,1024]{1,0:T(8,128)(2,1)} %get-tuple-element.110), channel_id=1, source_target_pairs={{0,2},{1,3},{2,0},{3,1},{4,6},{5,7},{6,4},{7,5},{8,10},{9,11},{10,... | collective-permute-start | bytes 393224 | tf_op jit(solution)/shard_map/ppermute | solution.py:473
  139.5 96.9 %collective-permute-start.17 = (bf16[256,1024]{1,0:T(8,128)(2,1)}, bf16[256,1024]{1,0:T(8,128)(2,1)}, u32[]{:S(2)}, u32[]{:S(2)}) collective-permute-start(bf16[256,1024]{1,0:T(8,128)(2,1)} %pad_maximum_fusion), channel_id=1, source_target_pairs={{0,2},{1,3},{2,0},{3,1},{4,6},{5,7},{6,4},{7,5},{8,10},{9,11},{10,... | collective-permute-start | bytes 1572872 | tf_op jit(solution)/shard_map/ppermute | solution.py:473
  140.7 93.8 %collective-permute-start.16 = (bf16[256,1024]{1,0:T(8,128)(2,1)}, bf16[256,1024]{1,0:T(8,128)(2,1)}, u32[]{:S(2)}, u32[]{:S(2)}) collective-permute-start(bf16[256,1024]{1,0:T(8,128)(2,1)} %pad_maximum_fusion), channel_id=1, source_target_pairs={{0,1},{1,2},{2,3},{3,0},{4,5},{5,6},{6,7},{7,4},{8,9},{9,10},{10,1... | collective-permute-start | bytes 1572872 | tf_op jit(solution)/shard_map/ppermute | solution.py:473
  145.6 80.8 %collective-permute-start.20 = (bf16[256,1024]{1,0:T(8,128)(2,1)}, bf16[256,1024]{1,0:T(8,128)(2,1)}, u32[]{:S(2)}, u32[]{:S(2)}) collective-permute-start(bf16[256,1024]{1,0:T(8,128)(2,1)} %get-tuple-element.106), channel_id=1, source_target_pairs={{0,2},{1,3},{2,0},{3,1},{4,6},{5,7},{6,4},{7,5},{8,10},{9,11},{10,... | collective-permute-start | bytes 1572872 | tf_op jit(solution)/shard_map/ppermute | solution.py:473
  148.1 41.3 %collective-permute-start.19 = (bf16[256,1024]{1,0:T(8,128)(2,1)}, bf16[256,1024]{1,0:T(8,128)(2,1)}, u32[]{:S(2)}, u32[]{:S(2)}) collective-permute-start(bf16[256,1024]{1,0:T(8,128)(2,1)} %get-tuple-element.106), channel_id=1, source_target_pairs={{0,1},{1,2},{2,3},{3,0},{4,5},{5,6},{6,7},{7,4},{8,9},{9,10},{10,1... | collective-permute-start | bytes 1572872 | tf_op jit(solution)/shard_map/ppermute | solution.py:473
  155.2 36.3 %collective-permute-start.14 = (bf16[256,1024]{1,0:T(8,128)(2,1)S(1)}, bf16[256,1024]{1,0:T(8,128)(2,1)S(1)}, u32[]{:S(2)}, u32[]{:S(2)}) collective-permute-start(bf16[256,1024]{1,0:T(8,128)(2,1)S(1)} %multiply_convert_fusion.2), channel_id=1, source_target_pairs={{0,8},{4,12},{8,0},{12,4},{16,24},{20,28},{24,16},{28,20},{1,9},{5... | collective-permute-start | bytes 1572872 | tf_op jit(solution)/shard_map/ppermute | solution.py:468
  189.4 44.3 %collective-permute-start.21 = (bf16[256,1024]{1,0:T(8,128)(2,1)}, bf16[256,1024]{1,0:T(8,128)(2,1)S(1)}, u32[]{:S(2)}, u32[]{:S(2)}) collective-permute-start(bf16[256,1024]{1,0:T(8,128)(2,1)} %get-tuple-element.106), channel_id=1, source_target_pairs={{0,3},{1,0},{2,1},{3,2},{4,7},{5,4},{6,5},{7,6},{8,11},{9,8},{10,9... | collective-permute-start | bytes 1572872 | tf_op jit(solution)/shard_map/ppermute | solution.py:473
  191.5 52.2 %collective-permute-start.18 = (bf16[256,1024]{1,0:T(8,128)(2,1)}, bf16[256,1024]{1,0:T(8,128)(2,1)S(1)}, u32[]{:S(2)}, u32[]{:S(2)}) collective-permute-start(bf16[256,1024]{1,0:T(8,128)(2,1)} %pad_maximum_fusion), channel_id=1, source_target_pairs={{0,3},{1,0},{2,1},{3,2},{4,7},{5,4},{6,5},{7,6},{8,11},{9,8},{10,9... | collective-permute-start | bytes 1572872 | tf_op jit(solution)/shard_map/ppermute | solution.py:473
  326.2 26.3 %collective-permute-start.56 = (bf16[4,128,1024]{1,2,0:T(8,128)(2,1)}, bf16[4,128,1024]{1,2,0:T(8,128)(2,1)}, u32[]{:S(2)}, u32[]{:S(2)}) collective-permute-start(bf16[4,128,1024]{1,2,0:T(8,128)(2,1)} %copy.146), channel_id=1, source_target_pairs={{0,16},{4,20},{8,24},{12,28},{16,0},{20,4},{24,8},{28,12},{1,17},{... | collective-permute-start | bytes 3145736 | tf_op jit(solution)/shard_map/ppermute | solution.py:468
  336.0 38.1 %collective-permute-start.49 = (bf16[4,128,1024]{1,2,0:T(8,128)(2,1)}, bf16[4,128,1024]{1,2,0:T(8,128)(2,1)}, u32[]{:S(2)}, u32[]{:S(2)}) collective-permute-start(bf16[4,128,1024]{1,2,0:T(8,128)(2,1)} %copy.144), channel_id=1, source_target_pairs={{0,16},{4,20},{8,24},{12,28},{16,0},{20,4},{24,8},{28,12},{1,17},{... | collective-permute-start | bytes 3145736 | tf_op jit(solution)/shard_map/ppermute | solution.py:468
  336.5 77.1 %collective-permute-start.24 = (bf16[256,1024]{1,0:T(8,128)(2,1)}, bf16[256,1024]{1,0:T(8,128)(2,1)}, u32[]{:S(2)}, u32[]{:S(2)}) collective-permute-start(bf16[256,1024]{1,0:T(8,128)(2,1)} %get-tuple-element.124), channel_id=1, source_target_pairs={{0,0},{8,1},{4,2},{12,3},{1,4},{9,5},{5,6},{13,7},{2,8},{10,9},{6,... | collective-permute-start | bytes 1572872 | tf_op jit(solution)/shard_map/ppermute | solution.py:808
  348.8 48.6 %collective-permute-start.29 = (bf16[256,1024]{1,0:T(8,128)(2,1)S(1)}, bf16[256,1024]{1,0:T(8,128)(2,1)S(1)}, u32[]{:S(2)}, u32[]{:S(2)}) collective-permute-start(bf16[256,1024]{1,0:T(8,128)(2,1)S(1)} %dynamic-slice_convert_fusion.5), channel_id=1, source_target_pairs={{0,8},{4,12},{8,0},{12,4},{16,24},{20,28},{24,16},{28,20},{1,9},{5... | collective-permute-start | bytes 1572872 | tf_op jit(solution)/shard_map/ppermute | solution.py:468
  354.0 26.0 %collective-permute-start.57 = (bf16[128,1024]{0,1:T(8,128)(2,1)S(1)}, bf16[128,1024]{0,1:T(8,128)(2,1)S(1)}, u32[]{:S(2)}, u32[]{:S(2)}) collective-permute-start(bf16[128,1024]{0,1:T(8,128)(2,1)S(1)} %get-tuple-element.125), channel_id=1, source_target_pairs={{0,1},{1,2},{2,3},{3,0},{4,5},{5,6},{6,7},{7,4},{8,9},{9,10},{10,1... | collective-permute-start | bytes 786440 | tf_op jit(solution)/shard_map/ppermute | solution.py:473
  435.9 48.1 %collective-permute-start.62 = (bf16[2,2,128,1024]{2,3,1,0:T(8,128)(2,1)}, bf16[2,2,128,1024]{2,3,1,0:T(8,128)(2,1)}, u32[]{:S(2)}, u32[]{:S(2)}) collective-permute-start(bf16[2,2,128,1024]{2,3,1,0:T(8,128)(2,1)} %maximum_select_fusion.14), channel_id=1, source_target_pairs={{0,4},{4,0},{8,12},{12,8},{16,20},{20,16},{24,28},{28,24},{1,5},{5... | collective-permute-start | bytes 3145736 | tf_op jit(solution)/shard_map/ppermute | solution.py:468
  444.5 33.9 %collective-permute-start.55 = (bf16[2,2,128,1024]{2,3,1,0:T(8,128)(2,1)}, bf16[2,2,128,1024]{2,3,1,0:T(8,128)(2,1)}, u32[]{:S(2)}, u32[]{:S(2)}) collective-permute-start(bf16[2,2,128,1024]{2,3,1,0:T(8,128)(2,1)} %maximum_select_fusion.12), channel_id=1, source_target_pairs={{0,4},{4,0},{8,12},{12,8},{16,20},{20,16},{24,28},{28,24},{1,5},{5... | collective-permute-start | bytes 3145736 | tf_op jit(solution)/shard_map/ppermute | solution.py:468
  470.7 39.3 %collective-permute-start.42 = (bf16[4,32,1024]{2,1,0:T(8,128)(2,1)S(1)}, bf16[4,32,1024]{2,1,0:T(8,128)(2,1)}, u32[]{:S(2)}, u32[]{:S(2)}) collective-permute-start(bf16[4,32,1024]{2,1,0:T(8,128)(2,1)S(1)} %constant_dynamic-slice_fusion.5), channel_id=1, source_target_pairs={{0,16},{4,20},{8,24},{12,28},{16,0},{20,4},{24,8},{28,12},{1,17},{... | collective-permute-start | bytes 786440 | tf_op jit(solution)/shard_map/ppermute | solution.py:468
  474.4 52.7 %collective-permute-start.35 = (bf16[4,128,768]{1,2,0:T(8,128)(2,1)}, bf16[4,128,768]{1,2,0:T(8,128)(2,1)}, u32[]{:S(2)}, u32[]{:S(2)}) collective-permute-start(bf16[4,128,768]{1,2,0:T(8,128)(2,1)} %copy.142), channel_id=1, source_target_pairs={{0,16},{4,20},{8,24},{12,28},{16,0},{20,4},{24,8},{28,12},{1,17},{... | collective-permute-start | bytes 2359304 | tf_op jit(solution)/shard_map/ppermute | solution.py:468
  478.4 70.1 %collective-permute-start.32 = (bf16[512,1024]{1,0:T(8,128)(2,1)S(1)}, bf16[512,1024]{1,0:T(8,128)(2,1)}, u32[]{:S(2)}, u32[]{:S(2)}) collective-permute-start(bf16[512,1024]{1,0:T(8,128)(2,1)S(1)} %dynamic-slice_convert_fusion), channel_id=1, source_target_pairs={{0,4},{4,0},{8,12},{12,8},{16,20},{20,16},{24,28},{28,24},{1,5},{5... | collective-permute-start | bytes 3145736 | tf_op jit(solution)/shard_map/ppermute | solution.py:468
  564.7 60.1 %collective-permute-start.41 = (bf16[2,2,128,768]{2,3,1,0:T(8,128)(2,1)}, bf16[2,2,128,768]{2,3,1,0:T(8,128)(2,1)}, u32[]{:S(2)}, u32[]{:S(2)}) collective-permute-start(bf16[2,2,128,768]{2,3,1,0:T(8,128)(2,1)} %maximum_select_fusion.16), channel_id=1, source_target_pairs={{0,4},{4,0},{8,12},{12,8},{16,20},{20,16},{24,28},{28,24},{1,5},{5... | collective-permute-start | bytes 2359304 | tf_op jit(solution)/shard_map/ppermute | solution.py:468
  570.9 52.9 %collective-permute-start.34 = (bf16[256,1024]{1,0:T(8,128)(2,1)}, bf16[256,1024]{1,0:T(8,128)(2,1)S(1)}, u32[]{:S(2)}, u32[]{:S(2)}) collective-permute-start(bf16[256,1024]{1,0:T(8,128)(2,1)} %fusion.21), channel_id=1, source_target_pairs={{0,0},{8,1},{4,2},{12,3},{1,4},{9,5},{5,6},{13,7},{2,8},{10,9},{6,... | collective-permute-start | bytes 1572872 | tf_op jit(solution)/shard_map/ppermute | solution.py:837
  (92 other events, 908.1 us)

commit v2 on v0

--- a/solution.py
+++ b/solution.py
@@ -1,8 +1,12 @@
+import functools
 import math
 
 import jax
 import jax.numpy as jnp
+import numpy as np
 from jax import lax
+from jax.experimental import pallas as pl
+from jax.experimental.pallas import tpu as pltpu
 from jax.sharding import PartitionSpec as P
 
 HEADS = 16
@@ -45,7 +49,7 @@
     return jnp.sum(values.astype(jnp.float32), axis=0)
 
 
-def per_device(
+def general_device(
     layer_input,
     query_weight,
     query_bias,
@@ -459,9 +463,831 @@
     )
 
 
+CORE, X, Y = 1, 2, 4
+GROUP = 4
+BLOCK = 256
+
+
+def swap(values, bit):
+    count = lax.axis_size("rep")
+    return lax.ppermute(values, "rep", [(i, i ^ bit) for i in range(count)])
+
+
+def shift(values, step):
+    count = lax.axis_size("shard")
+    return lax.ppermute(values, "shard", [(i, (i + step) % count) for i in range(count)])
+
+
+def token_pairs(count):
+    pairs = []
+    for rep in range(count):
+        for z in range(GROUP):
+            there = (rep & ~3) | ((z & 1) << 1) | (z >> 1)
+            pairs.append((rep * GROUP + z, there * GROUP + (rep & 3)))
+    return pairs
+
+
+def spot():
+    rep, place = lax.axis_index("rep"), lax.axis_index("shard")
+    return rep & 3, place, rep >> 2, ((rep >> 1) & 1) + 2 * (rep & 1)
+
+
+def aligned(index, size):
+    return pl.ds(pl.multiple_of(index * size, size), size)
+
+
+def dot(left, right):
+    return jnp.dot(left, right, preferred_element_type=jnp.float32)
+
+
+def nt(left, right):
+    return lax.dot_general(left, right, (((1,), (1,)), ((), ())), preferred_element_type=jnp.float32)
+
+
+def tn(left, right):
+    return lax.dot_general(left, right, (((0,), (0,)), ((), ())), preferred_element_type=jnp.float32)
+
+
+def rounded(values):
+    return values.astype(jnp.bfloat16)
+
+
+def wide(values):
+    return values.astype(jnp.float32)
+
+
+def shaped(*dims, kind=jnp.bfloat16):
+    return jax.ShapeDtypeStruct(dims, kind)
+
+
+VMEM_SPEC = pl.BlockSpec(memory_space=pltpu.VMEM)
+
+
+def call(kernel, outs, *operands, scratch=(), flops=0, exps=0, room=6):
+    size = lambda items: sum(math.prod(item.shape) * item.dtype.itemsize for item in items)
+    moved = size(operands) + size(outs)
+    spaces = [jax.ShapeDtypeStruct(item.shape, item.dtype) for item in scratch]
+    return pl.pallas_call(
+        kernel,
+        out_shape=tuple(outs),
+        in_specs=[VMEM_SPEC] * len(operands),
+        out_specs=tuple([VMEM_SPEC] * len(outs)),
+        scratch_shapes=list(scratch),
+        compiler_params=pltpu.CompilerParams(vmem_limit_bytes=moved + size(spaces) + (room << 20)),
+        cost_estimate=pl.CostEstimate(flops=flops, bytes_accessed=moved, transcendentals=exps),
+        name=kernel.__name__,
+    )(*operands)
+
+
+def standardize(values):
+    centered = values - jnp.mean(values, axis=-1, keepdims=True)
+    inverse = lax.rsqrt(jnp.mean(centered * centered, axis=-1, keepdims=True) + norm_epsilon)
+    return centered * inverse, inverse
+
+
+def turn(values, cosines, sines):
+    lane = lax.broadcasted_iota(jnp.int32, values.shape, 1)
+    swapped = jnp.where(lane % 64 < 32, pltpu.roll(values, 96, 1), pltpu.roll(values, 32, 1))
+    return values * cosines + swapped * sines
+
+
+def rope_tables(tokens, head_dim):
+    half = head_dim // 2
+    freqs = 10000.0 ** (-jnp.arange(half, dtype=jnp.float32) / half)
+    angles = jnp.arange(tokens, dtype=jnp.int32).astype(jnp.float32)[:, None] * freqs[None, :]
+    cosines, sines = jnp.cos(angles), jnp.sin(angles)
+    return (
+        jnp.concatenate([cosines] * 4, 1),
+        jnp.concatenate([-sines, sines, -sines, sines], 1),
+    )
+
+
+def pack_attention(
+    query_weight, key_weight, value_weight, out_weight, qb, kb, vb, ub, ob, db, ga, gb, gc, gd, packed
+):
+    quarter, place, _, _ = spot()
+    row = lax.broadcasted_iota(jnp.int32, (1024, 256), 0)
+    col = lax.broadcasted_iota(jnp.int32, (1024, 256), 1)
+    chosen = rounded(wide(row == (col // 64) * 256 + quarter * 64 + col % 64))
+    for index, weight in enumerate((query_weight, key_weight, value_weight)):
+        mine = rounded(dot(weight[...], chosen))
+        for half in range(2):
+            packed[half, :128, index * 256 : index * 256 + 256] = mine[half * 128 : half * 128 + 128]
+    out_mine = out_weight[aligned(quarter, 64), :]
+    for j in range(4):
+        at = (j % 2) * 64
+        packed[j // 2, at : at + 64, 768:1024] = out_mine[:, j * 256 : j * 256 + 256]
+    row = lax.broadcasted_iota(jnp.int32, (256, 256), 0)
+    col = lax.broadcasted_iota(jnp.int32, (256, 256), 1)
+    chosen = rounded(wide((row == quarter * 64 + col % 64) & (col // 64 == place)))
+    biases = [dot(jnp.broadcast_to(item[...][None, :], (16, 256)), chosen) for item in (qb, kb, vb)]
+    full = lambda item: jnp.broadcast_to(wide(item[...])[None, :], (16, 256))
+    up_mine = jnp.broadcast_to(wide(ub[aligned(quarter, 256)])[None, :], (16, 256))
+    zero = jnp.zeros((16, 256), jnp.float32)
+    first = jnp.concatenate(biases + [zero], 1)
+    second = jnp.concatenate([up_mine, full(ob), full(db), zero], 1)
+    third = jnp.concatenate([full(ga), full(gb), full(gc), full(gd)], 1)
+    at = lax.broadcasted_iota(jnp.int32, (16, 1024), 0)
+    rows = jnp.where(at == 0, first, jnp.where(at == 1, second, jnp.where(at == 2, third, 0.0)))
+    for half in range(2):
+        packed[half, 128:144, :] = rounded(rows)
+
+
+def pack_feed(up_weight, down_weight, up_packed, down_packed, sems):
+    quarter, _, _, _ = spot()
+    copies = []
+    for half in range(2):
+        for there in range(4):
+            lanes = pl.ds(pl.multiple_of(there * 1024 + quarter * 256, 256), 256)
+            copies.append(
+                (
+                    up_weight.at[half * 128 : half * 128 + 128, lanes],
+                    up_packed.at[half, :, there * 256 : there * 256 + 256],
+                )
+            )
+        copies.append((down_weight.at[aligned(quarter * 2 + half, 128), :], down_packed.at[half]))
+    copies = [pltpu.make_async_copy(a, b, sems.at[i]) for i, (a, b) in enumerate(copies)]
+    for copy in copies:
+        copy.start()
+    for copy in copies:
+        copy.wait()
+
+
+def call_pack_feed(up_weight, down_weight):
+    spec = pl.BlockSpec(memory_space=pl.ANY)
+    return pl.pallas_call(
+        pack_feed,
+        out_shape=(shaped(2, 128, 1024), shaped(2, 128, 1024)),
+        in_specs=[spec, spec],
+        out_specs=(VMEM_SPEC, VMEM_SPEC),
+        scratch_shapes=[pltpu.SemaphoreType.DMA((10,))],
+        compiler_params=pltpu.CompilerParams(vmem_limit_bytes=8 << 20),
+        cost_estimate=pl.CostEstimate(flops=0, bytes_accessed=2 << 20, transcendentals=0),
+        name="pack_feed",
+    )(up_weight, down_weight)
+
+
+def tie(value, *earlier):
+    return lax.optimization_barrier((value, *earlier))[0]
+
+
+def near_pieces(packed, half, *earlier):
+    mine = tie(lax.dynamic_index_in_dim(packed, half, 0, False), *earlier)
+    return [shift(mine, step) for step in (1, 2, 3)]
+
+
+def far_pieces(near):
+    return [swap(item, Y) for item in near]
+
+
+def each_piece(own, near, far):
+    _, place, y_bit, _ = spot()
+    yield place, 0, own.at[0]
+    yield place, 1, own.at[1]
+    for step in (1, 2, 3):
+        yield (place + 4 - step) & 3, y_bit, near[step - 1]
+        yield (place + 4 - step) & 3, 1 - y_bit, far[step - 1]
+
+
+def head_lanes(shape, parity):
+    return (lax.broadcasted_iota(jnp.int32, shape, 1) // 64) == parity
+
+
+def causal_block():
+    shape = (BLOCK, BLOCK)
+    return lax.broadcasted_iota(jnp.int32, shape, 0) >= lax.broadcasted_iota(jnp.int32, shape, 1)
+
+
+def attend(
+    x0, x1, x2, x3, own, z1, z2, z3, y1, y2, y3, cosines, sines,
+    query, key, value, mixed, logs, hidden, qkv, out_rows, vectors, p0, p1, p2, p3,
+):
+    _, _, _, position = spot()
+    for relative, rows_in in enumerate((x0, x1, x2, x3)):
+        hidden[aligned(position ^ relative, BLOCK), :] = rows_in[...]
+    vectors[...] = jnp.zeros_like(vectors)
+    for index, (shard, half, piece) in enumerate(each_piece(own, (z1, z2, z3), (y1, y2, y3))):
+        qkv[aligned(shard * 2 + half, 128), :] = piece[:128, :768]
+        for j in range(2):
+            out_rows[aligned(shard, 64), aligned(half * 2 + j, 256)] = piece[j * 64 : j * 64 + 64, 768:]
+        if index == 0 or index >= 2 and index % 2 == 0:
+            small = wide(piece[128:144, :])
+            lanes = aligned(shard, 256)
+            vectors[0:1, lanes] = small[1:2, 256:512]
+            vectors[1:2, lanes] = small[1:2, 512:768]
+            for gain in range(4):
+                vectors[2 + gain : 3 + gain, lanes] = small[2:3, gain * 256 : gain * 256 + 256]
+            vectors[6:7, lanes] = small[1:2, :256]
+            vectors[7:8, :] += small[0:1, :]
+
+    def project(index, carry):
+        rows = aligned(index, BLOCK)
+        normed, _ = standardize(wide(hidden[rows, :]))
+        block = rounded(normed * vectors[2:3, :])
+        hidden[rows, :] = block
+        raw = dot(block, qkv[...]) + vectors[7:8, :768]
+        cos, sin = cosines[rows, :], sines[rows, :]
+        for tile in range(2):
+            at = tile * 128
+            lanes = slice(at, at + 128)
+            query[rows, lanes] = rounded(turn(raw[:, lanes], cos, sin)) * jnp.bfloat16(0.125)
+            key[rows, lanes] = rounded(turn(raw[:, 256 + at : 384 + at], cos, sin))
+        value[rows, :] = rounded(raw[:, 512:])
+        return carry
+
+    lax.fori_loop(0, GROUP, project, 0)
+    causal = causal_block()
+    logs[...] = jnp.zeros_like(logs)
+
+    def pair_step(pair, carry):
+        lanes = aligned(pair, 128)
+        lane = lax.broadcasted_iota(jnp.int32, (BLOCK, 128), 1)
+        for block in range(GROUP):
+            rows = slice(block * BLOCK, block * BLOCK + BLOCK)
+            seen = (block + 1) * BLOCK
+            queries = query[rows, lanes]
+            keys, values = key[:seen, lanes], value[:seen, lanes]
+            outs = []
+            log_rows = logs[rows, :]
+            for parity in range(2):
+                masked = jnp.where(head_lanes(queries.shape, parity), queries, jnp.bfloat16(0))
+                scores = nt(masked, keys)
+                last = jnp.where(causal, scores[:, seen - BLOCK :], -1e30)
+                scores = jnp.concatenate([scores[:, : seen - BLOCK], last], 1) if block else last
+                best = jnp.max(scores, axis=1, keepdims=True)
+                exps = jnp.exp(scores - best)
+                total = jnp.sum(exps, axis=1, keepdims=True)
+                outs.append(dot(rounded(exps), values) / total)
+                log_rows = jnp.where(lane == pair * 2 + parity, best + jnp.log(total), log_rows)
+            mixed[rows, lanes] = rounded(jnp.where(lane < 64, outs[0], outs[1]))
+            logs[rows, :] = log_rows
+        return carry
+
+    lax.fori_loop(0, 2, pair_step, 0)
+    for relative, part in enumerate((p0, p1, p2, p3)):
+        part[...] = rounded(dot(mixed[aligned(position ^ relative, BLOCK), :], out_rows[...]))
+
+
+def attend_back(
+    a0, a1, a2, a3, out_rows, qkv, query, key, value, mixed, logs, cosines, sines,
+    grads, shift_sums, p0, p1, p2, p3, d_out, d_key, d_value, d_query,
+):
+    _, _, _, position = spot()
+    for relative, rows_in in enumerate((a0, a1, a2, a3)):
+        d_out[aligned(position ^ relative, BLOCK), :] = rounded(nt(rows_in[...], out_rows[...]))
+    d_key[...] = jnp.zeros_like(d_key)
+    d_value[...] = jnp.zeros_like(d_value)
+    causal = causal_block()
+
+    def pair_step(pair, carry):
+        lanes = aligned(pair, 128)
+        for block in range(GROUP):
+            rows = slice(block * BLOCK, block * BLOCK + BLOCK)
+            seen = (block + 1) * BLOCK
+            queries, d_outs = query[rows, lanes], d_out[rows, lanes]
+            keys, values = key[:seen, lanes], value[:seen, lanes]
+            products = wide(d_outs) * wide(mixed[rows, lanes])
+            log_rows = logs[rows, :]
+            lane = lax.broadcasted_iota(jnp.int32, (BLOCK, 128), 1)
+            d_queries = []
+            for parity in range(2):
+                mine = head_lanes((BLOCK, 128), parity)
+                masked_q = jnp.where(mine, queries, jnp.bfloat16(0))
+                masked_d = jnp.where(mine, d_outs, jnp.bfloat16(0))
+                log = jnp.sum(jnp.where(lane == pair * 2 + parity, log_rows, 0.0), 1, keepdims=True)
+                delta = jnp.sum(jnp.where(mine, products, 0.0), 1, keepdims=True)
+                probs = jnp.exp(nt(masked_q, keys) - log)
+                last = jnp.where(causal, probs[:, seen - BLOCK :], 0.0)
+                probs = jnp.concatenate([probs[:, : seen - BLOCK], last], 1) if block else last
+                d_scores = rounded(probs * (nt(masked_d, values) - delta))
+                d_queries.append(dot(d_scores, keys))
+                d_value[:seen, lanes] += tn(rounded(probs), masked_d)
+                d_key[:seen, lanes] += tn(d_scores, masked_q)
+            d_query[rows, lanes] = jnp.where(lane < 64, d_queries[0], d_queries[1])
+        return carry
+
+    lax.fori_loop(0, 2, pair_step, 0)
+    shift_sums[...] = jnp.zeros_like(shift_sums)
+
+    def finish(index, carry):
+        rows = aligned(index, BLOCK)
+        cos, sin = cosines[rows, :], -sines[rows, :]
+        for tile in range(2):
+            at = tile * 128
+            lanes = slice(at, at + 128)
+            grads[rows, at : at + 128] = rounded(turn(d_query[rows, lanes] * 0.125, cos, sin))
+            grads[rows, at + 256 : at + 384] = rounded(turn(d_key[rows, lanes], cos, sin))
+        grads[rows, 512:] = rounded(d_value[rows, :])
+        shift_sums[0:1, :] += jnp.sum(wide(grads[rows, :]), axis=0, keepdims=True)
+        return carry
+
+    lax.fori_loop(0, GROUP, finish, 0)
+    for relative, part in enumerate((p0, p1, p2, p3)):
+        part[...] = rounded(nt(grads[aligned(position ^ relative, BLOCK), :], qkv[...]))
+
+
+def after_attention(p0, core_in, x_in, rows_in, vectors, middle, hidden, normed_o, normed_f, inverses):
+    branch = wide(p0[...]) + wide(core_in[...]) + wide(x_in[...]) + vectors[0:1, :]
+    normed, inverse_o = standardize(branch)
+    normed_o[...] = normed
+    total = wide(rows_in[...]) + normed * vectors[3:4, :]
+    middle[...] = total
+    normed, inverse_f = standardize(total)
+    normed_f[...] = normed
+    hidden[...] = rounded(normed * vectors[4:5, :])
+    lane = lax.broadcasted_iota(jnp.int32, inverses.shape, 1)
+    inverses[...] = jnp.where(lane < 64, inverse_o, inverse_f)
+
+
+def after_feed(p0, core_in, x_in, middle, cotangent, vectors, layer_out, d_branch, sums):
+    branch = wide(p0[...]) + wide(core_in[...]) + wide(x_in[...]) + vectors[1:2, :]
+    normed, inverse = standardize(branch)
+    gain = vectors[5:6, :]
+    layer_out[...] = rounded(middle[...] + normed * gain)
+    upstream = wide(cotangent[...])
+    back = rounded(norm_back(normed, inverse, upstream * gain))
+    d_branch[...] = back
+    sums[...] = jnp.zeros_like(sums)
+    sums[0:1, :] = jnp.sum(upstream * normed, axis=0, keepdims=True)
+    sums[1:2, :] = jnp.sum(wide(back), axis=0, keepdims=True)
+
+
+def after_feed_back(
+    p0, core_in, x_in, cotangent, normed_o, normed_f, inverses, vectors, d_middle, d_branch, sums
+):
+    d_hidden = wide(p0[...]) + wide(core_in[...]) + wide(x_in[...])
+    normed = normed_f[...]
+    sums[...] = jnp.zeros_like(sums)
+    sums[0:1, :] = jnp.sum(d_hidden * normed, axis=0, keepdims=True)
+    total = wide(cotangent[...]) + norm_back(normed, inverses[:, 64:65], d_hidden * vectors[4:5, :])
+    d_middle[...] = total
+    normed = normed_o[...]
+    sums[1:2, :] = jnp.sum(total * normed, axis=0, keepdims=True)
+    back = rounded(norm_back(normed, inverses[:, 0:1], total * vectors[3:4, :]))
+    d_branch[...] = back
+    sums[2:3, :] = jnp.sum(wide(back), axis=0, keepdims=True)
+
+
+def after_attention_back(p0, core_in, x_in, rows_in, d_middle, vectors, d_rows, sums):
+    d_hidden = wide(p0[...]) + wide(core_in[...]) + wide(x_in[...])
+    normed, inverse = standardize(wide(rows_in[...]))
+    sums[...] = jnp.zeros_like(sums)
+    sums[0:1, :] = jnp.sum(d_hidden * normed, axis=0, keepdims=True)
+    d_rows[...] = rounded(d_middle[...] + norm_back(normed, inverse, d_hidden * vectors[2:3, :]))
+
+
+GELU_SCALE = math.sqrt(2.0 / math.pi)
+
+
+def feed_rows(rows_in, up_mat, down_mat, vectors, before, after, part, at):
+    rows = slice(at, at + BLOCK)
+
+    def step(index, carry):
+        lanes = aligned(index, BLOCK)
+        raw = dot(rows_in[...], up_mat[:, lanes]) + vectors[6:7, lanes]
+        before[rows, lanes] = raw
+        after[rows, lanes] = rounded(jax.nn.gelu(raw))
+        return carry
+
+    lax.fori_loop(0, 4, step, 0)
+
+    def out(index, carry):
+        lanes = aligned(index, BLOCK)
+        part[:, lanes] = rounded(dot(after[rows, :], down_mat[:, lanes]))
+        return carry
+
+    lax.fori_loop(0, 4, out, 0)
+
+
+def feed_first(
+    h0, h2, uo, u1, u2, u3, v1, v2, v3, do, d1, d2, d3, e1, e2, e3, vectors,
+    up_mat, down_mat, before, after, p0, p2,
+):
+    for shard, half, piece in each_piece(uo, (u1, u2, u3), (v1, v2, v3)):
+        up_mat[aligned(shard * 2 + half, 128), :] = piece[...]
+    for shard, half, piece in each_piece(do, (d1, d2, d3), (e1, e2, e3)):
+        down_mat[aligned(shard * 2 + half, 128), :] = piece[...]
+    feed_rows(h0, up_mat, down_mat, vectors, before, after, p0, 0)
+    feed_rows(h2, up_mat, down_mat, vectors, before, after, p2, BLOCK)
+
+
+def feed_second(h1, h3, up_mat, down_mat, vectors, before, after, p1, p3):
+    feed_rows(h3, up_mat, down_mat, vectors, before, after, p3, BLOCK)
+    feed_rows(h1, up_mat, down_mat, vectors, before, after, p1, 0)
+
+
+def feed_back(da, db, up_mat, down_mat, before, d_pre, pa, pb, sums):
+    sums[...] = jnp.zeros_like(sums)
+    for at, rows_in, part in ((BLOCK, db, pb), (0, da, pa)):
+        rows = slice(at, at + BLOCK)
+
+        def step(index, carry):
+            lanes = aligned(index, BLOCK)
+            upstream = nt(rows_in[...], down_mat[lanes, :])
+            raw = before[rows, lanes]
+            square = raw * raw
+            bent = jnp.tanh(GELU_SCALE * raw * (1.0 + 0.044715 * square))
+            slope = 0.5 * (1.0 + bent) + 0.5 * GELU_SCALE * raw * (1.0 - bent * bent) * (
+                1.0 + 3.0 * 0.044715 * square
+            )
+            back = rounded(upstream * slope)
+            d_pre[rows, lanes] = back
+            sums[0:1, lanes] += jnp.sum(wide(back), axis=0, keepdims=True)
+            return carry
+
+        lax.fori_loop(0, 4, step, 0)
+
+        def out(index, carry):
+            lanes = aligned(index, BLOCK)
+            part[:, lanes] = rounded(nt(d_pre[rows, :], up_mat[lanes, :]))
+            return carry
+
+        lax.fori_loop(0, 4, out, 0)
+
+
+def put_halves(keep, send, step, at, top, bottom):
+    _, _, y_bit, _ = spot()
+
+    @pl.when(y_bit == 0)
+    def _():
+        keep[step, at : at + 128, :] = top
+        send[step, at : at + 128, :] = bottom
+
+    @pl.when(y_bit == 1)
+    def _():
+        keep[step, at : at + 128, :] = bottom
+        send[step, at : at + 128, :] = top
+
+
+def down_grads(first, second, m0, m1, m2, m3, keep, send):
+    _, place, _, _ = spot()
+
+    def one(step, carry):
+        lanes = aligned((place + step) & 3, BLOCK)
+        down = (
+            tn(first[:BLOCK, lanes], m0[...])
+            + tn(first[BLOCK:, lanes], m2[...])
+            + tn(second[:BLOCK, lanes], m1[...])
+            + tn(second[BLOCK:, lanes], m3[...])
+        )
+        down = rounded(down)
+        put_halves(keep, send, step, 0, down[:128], down[128:])
+        return carry
+
+    lax.fori_loop(0, 4, one, 0)
+
+
+def up_grads(h0, h1, h2, h3, u_first, u_second, keep, send):
+    _, place, _, _ = spot()
+
+    def one(step, carry):
+        lanes = aligned((place + step) & 3, BLOCK)
+        up = (
+            tn(h0[:, lanes], u_first[:BLOCK, :])
+            + tn(h2[:, lanes], u_first[BLOCK:, :])
+            + tn(h1[:, lanes], u_second[:BLOCK, :])
+            + tn(h3[:, lanes], u_second[BLOCK:, :])
+        )
+        up = rounded(up)
+        put_halves(keep, send, step, 0, up[:128], up[128:])
+        return carry
+
+    lax.fori_loop(0, 4, one, 0)
+
+
+def attention_grads(mixed, a0, a1, a2, a3, hidden, d_qkv, keep, send, out_grad, block):
+    _, place, _, position = spot()
+    total = tn(mixed[aligned(position, BLOCK), :], a0[...])
+    for relative, rows_in in ((1, a1), (2, a2), (3, a3)):
+        total = total + tn(mixed[aligned(position ^ relative, BLOCK), :], rows_in[...])
+    out_grad[...] = rounded(total)
+
+    def one(step, carry):
+        shard = (place + step) & 3
+        block[:, :768] = rounded(tn(hidden[:, aligned(shard, BLOCK)], d_qkv[...]))
+        mine = out_grad[aligned(shard, 64), :]
+        for j in range(4):
+            block[j * 64 : j * 64 + 64, 768:] = mine[:, j * 256 : j * 256 + 256]
+        put_halves(keep, send, step, 0, block[:128, :], block[128:, :])
+        return carry
+
+    lax.fori_loop(0, 4, one, 0)
+
+
+def add_four(keep, come, s0, s1, s2, s3):
+    for step, out in enumerate((s0, s1, s2, s3)):
+        out[...] = rounded(wide(keep[step]) + wide(come[step]))
+
+
+def add_shards(s0, r1, r2, r3, total):
+    total[...] = rounded(wide(s0[...]) + wide(r1[...]) + wide(r2[...]) + wide(r3[...]))
+
+
+def each_part(own, x_part, y_part, core_part):
+    rep = lax.axis_index("rep")
+    refs = [own, x_part, y_part.at[0], y_part.at[1]] + [core_part.at[i] for i in range(4)]
+    for relative, ref in enumerate(refs):
+        flip = ((relative & 1) << 1) | ((relative & 2) << 1) | (relative >> 2)
+        there = rep ^ flip
+        yield there >> 2, there & 3, ref
+
+
+def unpack_down(own, x_part, y_part, core_part, down):
+    for y_bit, quarter, ref in each_part(own, x_part, y_part, core_part):
+        down[aligned(quarter * 2 + y_bit, 128), :] = wide(ref[...])
+
+
+def unpack_up(own, x_part, y_part, core_part, up):
+    for y_bit, quarter, ref in each_part(own, x_part, y_part, core_part):
+        for there in range(4):
+            lanes = pl.ds(pl.multiple_of(there * 1024 + quarter * 256, 256), 256)
+            up[aligned(y_bit, 128), lanes] = wide(ref[:, there * 256 : there * 256 + 256])
+
+
+def unpack_attention(own, x_part, y_part, core_part, query, key, value, out_weight):
+    rep = lax.axis_index("rep")
+    row = lax.broadcasted_iota(jnp.int32, (256, 1024), 0)
+    col = lax.broadcasted_iota(jnp.int32, (256, 1024), 1)
+    for out in (query, key, value):
+        out[...] = jnp.zeros_like(out)
+    for y_bit, quarter, ref in each_part(own, x_part, y_part, core_part):
+        chosen = rounded(wide(col == (row // 64) * 256 + quarter * 64 + row % 64))
+        for index, out in enumerate((query, key, value)):
+            out[aligned(y_bit, 128), :] += dot(ref[:, index * 256 : index * 256 + 256], chosen)
+        for j in range(2):
+            out_weight[aligned(quarter, 64), aligned(y_bit * 2 + j, 256)] = wide(
+                ref[j * 64 : j * 64 + 64, 768:]
+            )
+
+
+def reduce_y(keep, send):
+    part = shaped(keep.shape[1], 1024)
+    return call(add_four, [part] * 4, keep, swap(send, Y))
+
+
+def reduce_shards(parts):
+    s0, s1, s2, s3 = parts
+    (total,) = call(add_shards, [s0], s0, shift(s1, 1), shift(s2, 2), shift(s3, 3))
+    return total
+
+
+def gather_packs(total):
+    x_part = swap(total, X)
+    two = jnp.stack([total, x_part])
+    y_part = swap(two, Y)
+    return total, x_part, y_part, swap(jnp.concatenate([two, y_part]), CORE)
+
+
+def split_small(own, r1, r2, r3, *outs):
+    total = own[...] + r1[...] + r2[...] + r3[...]
+    for index, out in enumerate(outs):
+        if index < 9:
+            out[...] = total[:, index * 256 : index * 256 + 256]
+        else:
+            out[...] = total[:, 2304:]
+
+
+def fast_device(
+    layer_input,
+    query_weight,
+    query_bias,
+    key_weight,
+    key_bias,
+    value_weight,
+    value_bias,
+    output_weight,
+    output_bias,
+    up_weight,
+    up_bias,
+    down_weight,
+    down_bias,
+    attention_gain_in,
+    attention_gain_out,
+    feedforward_gain_in,
+    feedforward_gain_out,
+    layer_cotangent,
+):
+    f32, bf16 = jnp.float32, jnp.bfloat16
+    replicas = lax.axis_size("rep")
+    rows, width = layer_input.shape
+    tokens = rows * GROUP
+    quarter, place, y_bit, _ = spot()
+    pairs = token_pairs(replicas)
+    back_pairs = [(there, here) for here, there in pairs]
+    both = ("rep", "shard")
+    part = shaped(rows, width)
+    part32 = shaped(rows, width, kind=f32)
+    sums = shaped(8, width, kind=f32)
+
+    def spread(piece):
+        near, far = swap(piece, X), swap(piece, CORE)
+        return piece, near, far, swap(near, CORE)
+
+    def gather_sum(p1, p2, p3):
+        across = rounded(wide(p1) + wide(swap(p3, CORE)))
+        x_in = swap(across, X)
+        return swap(p2, CORE), x_in
+
+    own_rows = lax.ppermute(layer_input, both, pairs)
+    (packed,) = call(
+        pack_attention,
+        [shaped(2, 144, width)],
+        query_weight,
+        key_weight,
+        value_weight,
+        output_weight,
+        query_bias,
+        key_bias,
+        value_bias,
+        up_bias,
+        output_bias,
+        down_bias,
+        attention_gain_in,
+        attention_gain_out,
+        feedforward_gain_in,
+        feedforward_gain_out,
+    )
+    near_a = near_pieces(packed, y_bit)
+    cosines, sines = rope_tables(tokens, 64)
+    up_packed, down_packed = call_pack_feed(up_weight, down_weight)
+    own_rows = tie(own_rows, cosines, sines, up_packed)
+    blocks = spread(own_rows)
+    far_a = far_pieces(near_a)
+    near_u = near_pieces(up_packed, y_bit, *near_a)
+    near_d = near_pieces(down_packed, y_bit, *near_a)
+    head_rows = shaped(tokens, 256)
+    query, key, value, mixed, logs, hidden_a, qkv, out_rows, vectors, *parts = call(
+        attend,
+        [head_rows] * 4
+        + [
+            shaped(tokens, 128, kind=f32),
+            shaped(tokens, width),
+            shaped(width, 768),
+            shaped(256, width),
+            sums,
+        ]
+        + [part] * 4,
+        *blocks,
+        packed,
+        *near_a,
+        *far_a,
+        cosines,
+        sines,
+        flops=2 * tokens * 1024 * 1024 + 8 * tokens * tokens * 64 * 2,
+        exps=2 * tokens * tokens,
+        room=14,
+    )
+    core_in, x_in = gather_sum(*parts[1:])
+    far_u = far_pieces(near_u)
+    x_in = tie(x_in, *near_u)
+    middle, hidden_own, normed_o, normed_f, inverses = call(
+        after_attention,
+        [part32, part, part32, part32, shaped(rows, 128, kind=f32)],
+        parts[0],
+        core_in,
+        x_in,
+        own_rows,
+        vectors,
+    )
+    h0, h1, h2, h3 = spread(hidden_own)
+    far_d = far_pieces(near_d)
+    cotangent = lax.ppermute(tie(layer_cotangent, *near_d), both, pairs)
+    two32, two16 = shaped(2 * rows, width, kind=f32), shaped(2 * rows, width)
+    square = shaped(width, width)
+    flops = 4 * 2 * rows * 1024 * 1024
+    up_mat, down_mat, before_a, after_a, p0, p2 = call(
+        feed_first,
+        [square, square, two32, two16, part, part],
+        h0, h2, up_packed, *near_u, *far_u, down_packed, *near_d, *far_d, vectors,
+        flops=flops, room=10,
+    )
+    h1 = tie(h1, up_mat)
+    before_b, after_b, p1, p3 = call(
+        feed_second,
+        [two32, two16, part, part],
+        h1, h3, up_mat, down_mat, vectors,
+        flops=flops, room=10,
+    )
+    core_in, x_in = gather_sum(p1, p2, p3)
+    layer_output, d_branch, sums_f = call(
+        after_feed, [part, part, sums], p0, core_in, x_in, middle, cotangent, vectors
+    )
+    layer_output = lax.ppermute(layer_output, both, back_pairs)
+
+    m0, m1, m2, m3 = spread(d_branch)
+    u_first, p0, p2, sums_ua = call(
+        feed_back,
+        [two16, part, part, sums],
+        m0, m2, up_mat, down_mat, before_a,
+        flops=flops, room=10,
+    )
+    m1 = tie(m1, u_first)
+    u_second, p1, p3, sums_ub = call(
+        feed_back,
+        [two16, part, part, sums],
+        m1, m3, up_mat, down_mat, before_b,
+        flops=flops, room=10,
+    )
+    core_in, x_in = gather_sum(p1, p2, p3)
+    packs = [shaped(4, 128, width)] * 2
+    flops = 2 * tokens * 1024 * 1024
+    pack_d = call(down_grads, packs, after_a, after_b, m0, m1, m2, m3, flops=flops, room=10)
+    pack_u = call(up_grads, packs, h0, h1, h2, h3, u_first, u_second, flops=flops, room=10)
+    x_in = tie(x_in, *pack_d, *pack_u)
+    d_middle, d_branch, sums_b = call(
+        after_feed_back,
+        [part32, part, sums],
+        p0,
+        core_in,
+        x_in,
+        cotangent,
+        normed_o,
+        normed_f,
+        inverses,
+        vectors,
+    )
+    a0, a1, a2, a3 = spread(d_branch)
+    parts_d = reduce_y(*pack_d)
+    a1 = tie(a1, layer_output, *parts_d)
+    a_blocks = a0, a1, a2, a3
+    grad32 = pltpu.VMEM((tokens, 256), f32)
+    d_qkv, sums_q, p0, p1, p2, p3 = call(
+        attend_back,
+        [shaped(tokens, 768), shaped(8, 768, kind=f32)] + [part] * 4,
+        *a_blocks, out_rows, qkv, query, key, value, mixed, logs, cosines, sines,
+        scratch=[pltpu.VMEM((tokens, 256), bf16), grad32, grad32, grad32],
+        flops=2 * tokens * 1024 * 1024 + 20 * tokens * tokens * 64 * 2,
+        exps=2 * tokens * tokens,
+        room=14,
+    )
+    core_in, x_in = gather_sum(p1, p2, p3)
+    pack_a = call(
+        attention_grads,
+        packs,
+        mixed, *a_blocks, hidden_a, d_qkv,
+        scratch=[pltpu.VMEM((256, width), bf16), pltpu.VMEM((256, width), bf16)],
+        flops=flops,
+        room=10,
+    )
+    parts_u = reduce_y(*pack_u)
+    total_d = reduce_shards(parts_d)
+    x_in = tie(x_in, *pack_a, total_d)
+    input_gradient, sums_a = call(
+        after_attention_back, [part, sums], p0, core_in, x_in, own_rows, d_middle, vectors
+    )
+    input_gradient = lax.ppermute(input_gradient, both, back_pairs).astype(f32)
+    parts_a = reduce_y(*pack_a)
+    total_u = reduce_shards(parts_u)
+    total_a = reduce_shards(parts_a)
+    (g_down,) = call(unpack_down, [shaped(*down_weight.shape, kind=f32)], *gather_packs(total_d))
+    (g_up,) = call(unpack_up, [shaped(*up_weight.shape, kind=f32)], *gather_packs(total_u))
+    g_query, g_key, g_value, g_out = call(unpack_attention, [part32] * 4, *gather_packs(total_a))
+
+    def local(values, size):
+        out = jnp.zeros((4, 4, size), f32)
+        return lax.dynamic_update_slice(out, values.reshape(4, 1, size), (0, quarter, 0)).reshape(4, -1)
+
+    per = width // 4
+    vector = [local(sums_q[0, i * 256 : (i + 1) * 256], 64) for i in range(3)]
+    for item in (sums_b[2], sums_f[1], sums_a[0], sums_b[1], sums_b[0], sums_f[0]):
+        vector.append(item.reshape(4, per))
+    vector.append(local(sums_ua[0] + sums_ub[0], 256))
+    vector = jnp.concatenate(vector, 1)
+    for bit in (CORE, X, Y):
+        vector = vector + swap(vector, bit)
+    pieces = [lax.dynamic_index_in_dim(vector, (place + step) % 4, 0, True) for step in range(4)]
+    pieces = [pieces[0]] + [shift(pieces[step], step) for step in (1, 2, 3)]
+    small = call(
+        split_small, [shaped(1, 256, kind=f32)] * 9 + [shaped(1, 1024, kind=f32)], *pieces
+    )
+    small = [item.reshape(-1) for item in small]
+    return (
+        layer_output,
+        input_gradient,
+        g_query,
+        small[0],
+        g_key,
+        small[1],
+        g_value,
+        small[2],
+        g_out,
+        small[3],
+        g_up,
+        small[9],
+        g_down,
+        small[4],
+        small[5],
+        small[6],
+        small[7],
+        small[8],
+    )
+
+
 def solution(mesh):
+    replicas, shards = mesh.shape["rep"], mesh.shape["shard"]
+    fits = shards == 4 and replicas == 8 and HEADS % 16 == 0
     return jax.shard_map(
-        per_device,
+        fast_device if fits else general_device,
         mesh=mesh,
         in_specs=(
             P(("rep", "shard"), None),

time: 1370 us -> 457 us (0.33)
  waiting for transfers between devices: 1020 us -> 221 us
  blocking collectives: 125 us -> 0 us
  starting transfers between devices: 1.06 us -> 121 us
  matrix products: 119 us -> 0 us
  Pallas kernels: 0 us -> 83.6 us
  local copies, waits for them, and re-layouts: 40.1 us -> 7.8 us
  other arithmetic: 44.1 us -> 13.7 us
  between operations: 16.3 us -> 1.86 us
    reduce_scatter x8 -> x0, waiting for transfers between devices: 533 us -> none  [the longest x1 147 us: per_device(): lax.psum_scatter(grad_down.astype(jnp.bfloat16), 'shard', scatter_dimensi...]
    all_gather x8 -> x0, waiting for transfers between devices: 414 us -> none  [the longest x1 145 us: per_device(): lax.all_gather(feed_local[0], 'shard', axis=0, tiled=True)]
    ppermute x0 -> x73, waiting for transfers between devices: none -> 221 us  [the longest x48 151 us: swap(): return lax.ppermute(values, 'rep', [(i, i ^ bit) for i in range(count)])]
    ppermute x0 -> x73, starting transfers between devices: none -> 121 us  [the longest x48 60.8 us: swap(): return lax.ppermute(values, 'rep', [(i, i ^ bit) for i in range(count)])]
    dot_general x32 -> x0, matrix products: 119 us -> none  [the longest x2 11 us: backward_inner(): jnp.einsum('hqk,qhd->khd', probs.astype(jnp.bfloat16), d_heads, preferred...]
    all_gather x10 -> x0, blocking collectives: 93.4 us -> none  [the longest x1 12.6 us: per_device(): lax.all_gather(attention_local[8], 'shard', axis=0, tiled=True)]
    pallas_call x0 -> x25, Pallas kernels: none -> 83.6 us  [the longest x24 83.4 us: call(): pl.pallas_call(kernel, out_shape=tuple(outs), in_specs=[VMEM_SPEC] * len(...]
    psum x1 -> x0, waiting for transfers between devices: 64.2 us -> none  [per_device(): lax.psum(g_query.astype(jnp.bfloat16), 'rep').astype(jnp.float32)]
  transfers between devices with their start and end apart: 17 -> 73, of which waited for: 16 -> 30; matrix products, arithmetic and copies ran while one was open for 8% -> 3% of each run, Pallas kernels for 0% -> 12%
where the time goes in v2:
time: 457 us; the launch traced here: 448 us
  waiting for transfers between devices  221 us (48%)
  starting transfers between devices  121 us (26%)
  Pallas kernels  83.6 us (18%)
  other arithmetic  13.7 us (3%)
  local copies, waits for them, and re-layouts  7.8 us (2%)
    ppermute x48, waiting for transfers between devices, swap(): return lax.ppermute(values, 'rep', [(i, i ^ bit) for i in range(count)])  151 us
    pallas_call x24, Pallas kernels, call(): pl.pallas_call(kernel, out_shape=tuple(outs), in_specs=[VMEM_SPEC] * len(...  83.4 us
    ppermute x21, waiting for transfers between devices, shift(): lax.ppermute(values, 'shard', [(i, (i + step) % count) for i in range(cou...  69.8 us
    ppermute x48, starting transfers between devices, swap(): return lax.ppermute(values, 'rep', [(i, i ^ bit) for i in range(count)])  60.8 us
    ppermute x21, starting transfers between devices, shift(): lax.ppermute(values, 'shard', [(i, (i + step) % count) for i in range(cou...  51.1 us
  transfers between devices with their start and end apart: 73, of which 30 were waited for; matrix products, arithmetic and copies ran while one was open for 3% of the time, Pallas kernels for 12%

profile of v2, /device:TPU:0, one launch (start us, length us, event | category | flops | bytes accessed | tf_op | source)
XLA Modules:
  0.0 448.1 jit_solution(1594278730778687243)
XLA Ops:
  9.6 11.4 %collective-permute-start.1 = (bf16[256,1024]{1,0:T(8,128)(2,1)S(1)}, bf16[256,1024]{1,0:T(8,128)(2,1)}, u32[]{:S(2)}, u32[]{:S(2)}) collective-permute-start(bf16[256,1024]{1,0:T(8,128)(2,1)S(1)} %collective-permute-done.x0.rows_in), channel_id=1, source_target_pairs={{0,8},{4,12},{8,0},{12,4},{16,24},{20,28},{24,16},{28,20},{1,9},{5... | collective-permute-start | bytes 1572872 | tf_op jit(solution)/shard_map/ppermute | solution.py:473
  21.9 11.2 %collective-permute-start.4 = (bf16[144,1024]{1,0:T(8,128)(2,1)S(1)}, bf16[144,1024]{1,0:T(8,128)(2,1)S(1)}, u32[]{:S(2)}, u32[]{:S(2)}) collective-permute-start(bf16[144,1024]{1,0:T(8,128)(2,1)S(1)} %dynamic-slice_bitcast_fusion), channel_id=1, source_target_pairs={{0,1},{1,2},{2,3},{3,0},{4,5},{5,6},{6,7},{7,4},{8,9},{9,10},{10,1... | collective-permute-start | bytes 884744 | tf_op jit(solution)/shard_map/ppermute | solution.py:478
  38.3 5.9 %collective-permute-done.4.z1 = bf16[144,1024]{1,0:T(8,128)(2,1)S(1)} collective-permute-done((bf16[144,1024]{1,0:T(8,128)(2,1)S(1)}, bf16[144,1024]{1,0:T(8,128)(2,1)S(1)}, u32[]{:S(2)}, u32[]{:S(2)}) %collective-permute-start.4) | collective-permute-done | bytes 294944 | tf_op jit(solution)/shard_map/ppermute | solution.py:478
  45.8 8.6 %collective-permute-done.5.z2 = bf16[144,1024]{1,0:T(8,128)(2,1)S(1)} collective-permute-done((bf16[144,1024]{1,0:T(8,128)(2,1)S(1)}, bf16[144,1024]{1,0:T(8,128)(2,1)S(1)}, u32[]{:S(2)}, u32[]{:S(2)}) %collective-permute-start.5) | collective-permute-done | bytes 294944 | tf_op jit(solution)/shard_map/ppermute | solution.py:478
  56.4 7.9 %collective-permute-done.8.y2 = bf16[144,1024]{1,0:T(8,128)(2,1)S(1)} collective-permute-done((bf16[144,1024]{1,0:T(8,128)(2,1)S(1)}, bf16[144,1024]{1,0:T(8,128)(2,1)S(1)}, u32[]{:S(2)}, u32[]{:S(2)}) %collective-permute-start.8) | collective-permute-done | bytes 294944 | tf_op jit(solution)/shard_map/ppermute | solution.py:473
  69.5 12.8 %attend.1 = (bf16[1024,256]{1,0:T(8,128)(2,1)S(1)}, bf16[1024,256]{1,0:T(8,128)(2,1)S(1)}, bf16[1024,256]{1,0:T(8,128)(2,1)S(1)}, bf16[1024,256]{1,0:T(8,128)(2,...) custom-call(bf16[256,1024]{1,0:T(8,128)(2,1)S(1)} %collective-permut, ...), custom_call_target="tpu_custom_call" | custom-call | flops 3221225472 | bytes 14450688 | tf_op jit(solution)/shard_map/attend/pallas_call | solution.py:530
  97.2 11.0 %collective-permute-done.14.u2 = bf16[128,1024]{1,0:T(8,128)(2,1)S(1)} collective-permute-done((bf16[128,1024]{1,0:T(8,128)(2,1)S(1)}, bf16[128,1024]{1,0:T(8,128)(2,1)S(1)}, u32[]{:S(2)}, u32[]{:S(2)}) %collective-permute-start.14) | collective-permute-done | bytes 262176 | tf_op jit(solution)/shard_map/ppermute | solution.py:478
  110.6 6.1 %collective-permute-start.20 = (bf16[128,1024]{1,0:T(8,128)(2,1)S(1)}, bf16[128,1024]{1,0:T(8,128)(2,1)S(1)}, u32[]{:S(2)}, u32[]{:S(2)}) collective-permute-start(bf16[128,1024]{1,0:T(8,128)(2,1)S(1)} %get-tuple-element.123), channel_id=1, source_target_pairs={{0,1},{1,2},{2,3},{3,0},{4,5},{5,6},{6,7},{7,4},{8,9},{9,10},{10,1... | collective-permute-start | bytes 786440 | tf_op jit(solution)/shard_map/ppermute | solution.py:478
  127.7 8.6 %collective-permute-done.21.d2 = bf16[128,1024]{1,0:T(8,128)(2,1)S(1)} collective-permute-done((bf16[128,1024]{1,0:T(8,128)(2,1)S(1)}, bf16[128,1024]{1,0:T(8,128)(2,1)S(1)}, u32[]{:S(2)}, u32[]{:S(2)}) %collective-permute-start.21) | collective-permute-done | bytes 262176 | tf_op jit(solution)/shard_map/ppermute | solution.py:478
  151.1 5.6 %collective-permute-done.24.e2 = bf16[128,1024]{1,0:T(8,128)(2,1)S(1)} collective-permute-done((bf16[128,1024]{1,0:T(8,128)(2,1)S(1)}, bf16[128,1024]{1,0:T(8,128)(2,1)S(1)}, u32[]{:S(2)}, u32[]{:S(2)}) %collective-permute-start.24) | collective-permute-done | bytes 262176 | tf_op jit(solution)/shard_map/ppermute | solution.py:473
  161.3 5.7 %feed_first.1 = (bf16[1024,1024]{1,0:T(8,128)(2,1)S(1)}, bf16[1024,1024]{1,0:T(8,128)(2,1)S(1)}, f32[512,1024]{1,0:T(8,128)S(1)}, bf16[512,1024]{1,0:T(8,128)(2,...) custom-call(bf16[256,1024]{1,0:T(8,128)(2,1)S(1)} %get-tuple-element.121.h0, ...), custom_call_target="tpu_custom_call" | custom-call | flops 2147483648 | bytes 13664256 | tf_op jit(solution)/shard_map/feed_first/pallas_call | solution.py:530
  181.5 19.4 %collective-permute-done.30.x_in = bf16[256,1024]{1,0:T(8,128)(2,1)S(1)} collective-permute-done((bf16[256,1024]{1,0:T(8,128)(2,1)S(1)}, bf16[256,1024]{1,0:T(8,128)(2,1)S(1)}, u32[]{:S(2)}, u32[]{:S(2)}) %collective-permute-start.30) | collective-permute-done | bytes 524320 | tf_op jit(solution)/shard_map/ppermute | solution.py:473
  204.6 12.1 %collective-permute-done.35.da.m1 = bf16[256,1024]{1,0:T(8,128)(2,1)S(1)} collective-permute-done((bf16[256,1024]{1,0:T(8,128)(2,1)S(1)}, bf16[256,1024]{1,0:T(8,128)(2,1)S(1)}, u32[]{:S(2)}, u32[]{:S(2)}) %collective-permute-start.35) | collective-permute-done | bytes 524320 | tf_op jit(solution)/shard_map/ppermute | solution.py:473
  216.7 5.9 %feed_back.2 = (bf16[512,1024]{1,0:T(8,128)(2,1)S(1)}, bf16[256,1024]{1,0:T(8,128)(2,1)S(1)}, bf16[256,1024]{1,0:T(8,128)(2,1)S(1)}, f32[8,1024]{1,0:T(8,128)S(1)}) custom-call(bf16[256,1024]{1,0:T(8,128)(2,1)S(1)} %get-tuple-element.134.da.m0, bf16[256,1024]{1,0:T(8,128)(2,1)S(1)} %collective-permute-done.33.db.m2, ...), custom_call_target="tpu_custom_call" | custom-call | flops 2147483648 | bytes 9469952 | tf_op jit(solution)/shard_map/feed_back/pallas_call | solution.py:530
  222.6 5.9 %feed_back.3 = (bf16[512,1024]{1,0:T(8,128)(2,1)S(1)}, bf16[256,1024]{1,0:T(8,128)(2,1)S(1)}, bf16[256,1024]{1,0:T(8,128)(2,1)S(1)}, f32[8,1024]{1,0:T(8,128)S(1)}) custom-call(bf16[256,1024]{1,0:T(8,128)(2,1)S(1)} %collective-permute-done.35.da.m1, bf16[256,1024]{1,0:T(8,128)(2,1)S(1)} %collective-permute-done.36.db.m3, ...), custom_call_target="tpu_custom_call" | custom-call | flops 2147483648 | bytes 9469952 | tf_op jit(solution)/shard_map/feed_back/pallas_call | solution.py:530
  239.6 8.1 %collective-permute-done.38.x_in = bf16[256,1024]{1,0:T(8,128)(2,1)S(1)} collective-permute-done((bf16[256,1024]{1,0:T(8,128)(2,1)S(1)}, bf16[256,1024]{1,0:T(8,128)(2,1)S(1)}, u32[]{:S(2)}, u32[]{:S(2)}) %collective-permute-start.38) | collective-permute-done | bytes 524320 | tf_op jit(solution)/shard_map/ppermute | solution.py:473
  250.9 7.5 %collective-permute-done.63.come = bf16[4,128,1024]{2,1,0:T(8,128)(2,1)S(1)} collective-permute-done((bf16[4,128,1024]{2,1,0:T(8,128)(2,1)S(1)}, bf16[4,128,1024]{2,1,0:T(8,128)(2,1)S(1)}, u32[]{:S(2)}, u32[]{:S(2)}) %collective-permute-start.63) | collective-permute-done | bytes 1048608 | tf_op jit(solution)/shard_map/ppermute | solution.py:473
  264.8 15.1 %collective-permute-done.40.come = bf16[4,128,1024]{2,1,0:T(8,128)(2,1)S(1)} collective-permute-done((bf16[4,128,1024]{2,1,0:T(8,128)(2,1)S(1)}, bf16[4,128,1024]{2,1,0:T(8,128)(2,1)S(1)}, u32[]{:S(2)}, u32[]{:S(2)}) %collective-permute-start.40) | collective-permute-done | bytes 1048608 | tf_op jit(solution)/shard_map/ppermute | solution.py:473
  283.5 11.2 %collective-permute-done.65.r2 = bf16[128,1024]{1,0:T(8,128)(2,1)S(1)} collective-permute-done((bf16[128,1024]{1,0:T(8,128)(2,1)S(1)}, bf16[128,1024]{1,0:T(8,128)(2,1)S(1)}, u32[]{:S(2)}, u32[]{:S(2)}) %collective-permute-start.65) | collective-permute-done | bytes 262176 | tf_op jit(solution)/shard_map/ppermute | solution.py:478
  303.8 13.4 %attend_back.1 = (bf16[1024,768]{1,0:T(8,128)(2,1)S(1)}, f32[8,768]{1,0:T(8,128)S(1)}, bf16[256,1024]{1,0:T(8,128)(2,1)S(1)}, bf16[256,1024]{1,0:T(8,128)(2,1)S(...) custom-call(bf16[256,1024]{1,0:T(8,128)(2,1)S(1)} %get-tuple-element.154.a0, ...), custom_call_target="tpu_custom_call" | custom-call | flops 4831838208 | bytes 11558912 | tf_op jit(solution)/shard_map/attend_back/pallas_call | solution.py:530
  333.2 27.1 %collective-permute-done.68.y_part = bf16[2,128,1024]{2,1,0:T(8,128)(2,1)S(1)} collective-permute-done((bf16[2,128,1024]{2,1,0:T(8,128)(2,1)S(1)}, bf16[2,128,1024]{2,1,0:T(8,128)(2,1)S(1)}, u32[]{:S(2)}, u32[]{:S(2)}) %collective-permute-start.68) | collective-permute-done | bytes 524320 | tf_op jit(solution)/shard_map/ppermute | solution.py:473
  374.8 6.7 %collective-permute-done.52.r2 = bf16[128,1024]{1,0:T(8,128)(2,1)S(1)} collective-permute-done((bf16[128,1024]{1,0:T(8,128)(2,1)}, bf16[128,1024]{1,0:T(8,128)(2,1)S(1)}, u32[]{:S(2)}, u32[]{:S(2)}) %collective-permute-start.52) | collective-permute-done | bytes 262176 | tf_op jit(solution)/shard_map/ppermute | solution.py:478
  395.9 8.4 %collective-permute-done.45.x_in = bf16[256,1024]{1,0:T(8,128)(2,1)S(1)} collective-permute-done((bf16[256,1024]{1,0:T(8,128)(2,1)S(1)}, bf16[256,1024]{1,0:T(8,128)(2,1)S(1)}, u32[]{:S(2)}, u32[]{:S(2)}) %collective-permute-start.45) | collective-permute-done | bytes 524320 | tf_op jit(solution)/shard_map/ppermute | solution.py:473
  440.9 6.0 %unpack_attention.1 = (f32[256,1024]{1,0:T(8,128)}, f32[256,1024]{1,0:T(8,128)}, f32[256,1024]{1,0:T(8,128)}, f32[256,1024]{1,0:T(8,128)}) custom-call(bf16[128,1024]{1,0:T(8,128)(2,1)S(1)} %add_shards.4.own, bf16[128,1024]{1,0:T(8,128)(2,1)S(1)} %collective-permute-done.54.x_part, bf16[2,128,1024]{2,1,0:T(8,128)(2,1)} %collective-permute-done.55.y_part, ...), custom_call_target="tpu_custom_call" | custom-call | bytes 6291456 | tf_op jit(solution)/shard_map/unpack_attention/pallas_call | solution.py:530
  (273 shorter events, 204.5 us)
Async XLA Ops:
  9.6 28.2 %collective-permute-start.1 = (bf16[256,1024]{1,0:T(8,128)(2,1)S(1)}, bf16[256,1024]{1,0:T(8,128)(2,1)}, u32[]{:S(2)}, u32[]{:S(2)}) collective-permute-start(bf16[256,1024]{1,0:T(8,128)(2,1)S(1)} %collective-permute-done.x0.rows_in), channel_id=1, source_target_pairs={{0,8},{4,12},{8,0},{12,4},{16,24},{20,28},{24,16},{28,20},{1,9},{5... | collective-permute-start | bytes 1572872 | tf_op jit(solution)/shard_map/ppermute | solution.py:473
  37.8 31.7 %collective-permute-start.2 = (bf16[256,1024]{1,0:T(8,128)(2,1)S(1)}, bf16[256,1024]{1,0:T(8,128)(2,1)S(1)}, u32[]{:S(2)}, u32[]{:S(2)}) collective-permute-start(bf16[256,1024]{1,0:T(8,128)(2,1)S(1)} %collective-permute-done.x0.rows_in), channel_id=1, source_target_pairs={{0,4},{4,0},{8,12},{12,8},{16,20},{20,16},{24,28},{28,24},{1,5},{5... | collective-permute-start | bytes 1572872 | tf_op jit(solution)/shard_map/ppermute | solution.py:473
  37.8 31.7 %collective-permute-start.3 = (bf16[256,1024]{1,0:T(8,128)(2,1)}, bf16[256,1024]{1,0:T(8,128)(2,1)S(1)}, u32[]{:S(2)}, u32[]{:S(2)}) collective-permute-start(bf16[256,1024]{1,0:T(8,128)(2,1)} %collective-permute-done.1.x1), channel_id=1, source_target_pairs={{0,4},{4,0},{8,12},{12,8},{16,20},{20,16},{24,28},{28,24},{1,5},{5... | collective-permute-start | bytes 1572872 | tf_op jit(solution)/shard_map/ppermute | solution.py:473
  84.5 23.7 %collective-permute-start.12 = (bf16[256,1024]{1,0:T(8,128)(2,1)S(1)}, bf16[256,1024]{1,0:T(8,128)(2,1)S(1)}, u32[]{:S(2)}, u32[]{:S(2)}) collective-permute-start(bf16[256,1024]{1,0:T(8,128)(2,1)S(1)} %add_convert_fusion.3), channel_id=1, source_target_pairs={{0,8},{4,12},{8,0},{12,4},{16,24},{20,28},{24,16},{28,20},{1,9},{5... | collective-permute-start | bytes 1572872 | tf_op jit(solution)/shard_map/ppermute | solution.py:473
  109.1 28.7 %collective-permute-start.27 = (bf16[256,1024]{1,0:T(8,128)(2,1)S(1)}, bf16[256,1024]{1,0:T(8,128)(2,1)S(1)}, u32[]{:S(2)}, u32[]{:S(2)}) collective-permute-start(bf16[256,1024]{1,0:T(8,128)(2,1)S(1)} %get-tuple-element.121.h0), channel_id=1, source_target_pairs={{0,8},{4,12},{8,0},{12,4},{16,24},{20,28},{24,16},{28,20},{1,9},{5... | collective-permute-start | bytes 1572872 | tf_op jit(solution)/shard_map/ppermute | solution.py:473
  137.8 23.5 %collective-permute-start.16 = (bf16[256,1024]{1,0:T(8,128)(2,1)S(1)}, bf16[256,1024]{1,0:T(8,128)(2,1)S(1)}, u32[]{:S(2)}, u32[]{:S(2)}) collective-permute-start(bf16[256,1024]{1,0:T(8,128)(2,1)S(1)} %get-tuple-element.121.h0), channel_id=1, source_target_pairs={{0,4},{4,0},{8,12},{12,8},{16,20},{20,16},{24,28},{28,24},{1,5},{5... | collective-permute-start | bytes 1572872 | tf_op jit(solution)/shard_map/ppermute | solution.py:473
  137.8 29.2 %collective-permute-start.28 = (bf16[256,1024]{1,0:T(8,128)(2,1)S(1)}, bf16[256,1024]{1,0:T(8,128)(2,1)S(1)}, u32[]{:S(2)}, u32[]{:S(2)}) collective-permute-start(bf16[256,1024]{1,0:T(8,128)(2,1)S(1)} %collective-permute-done.27.h1), channel_id=1, source_target_pairs={{0,4},{4,0},{8,12},{12,8},{16,20},{20,16},{24,28},{28,24},{1,5},{5... | collective-permute-start | bytes 1572872 | tf_op jit(solution)/shard_map/ppermute | solution.py:473
  177.2 23.8 %collective-permute-start.30 = (bf16[256,1024]{1,0:T(8,128)(2,1)S(1)}, bf16[256,1024]{1,0:T(8,128)(2,1)S(1)}, u32[]{:S(2)}, u32[]{:S(2)}) collective-permute-start(bf16[256,1024]{1,0:T(8,128)(2,1)S(1)} %add_convert_fusion.2), channel_id=1, source_target_pairs={{0,8},{4,12},{8,0},{12,4},{16,24},{20,28},{24,16},{28,20},{1,9},{5... | collective-permute-start | bytes 1572872 | tf_op jit(solution)/shard_map/ppermute | solution.py:473
  232.3 26.1 %collective-permute-start.63 = (bf16[4,128,1024]{2,1,0:T(8,128)(2,1)S(1)}, bf16[4,128,1024]{2,1,0:T(8,128)(2,1)S(1)}, u32[]{:S(2)}, u32[]{:S(2)}) collective-permute-start(bf16[4,128,1024]{2,1,0:T(8,128)(2,1)S(1)} %get-tuple-element.149), channel_id=1, source_target_pairs={{0,16},{4,20},{8,24},{12,28},{16,0},{20,4},{24,8},{28,12},{1,17},{... | collective-permute-start | bytes 3145736 | tf_op jit(solution)/shard_map/ppermute | solution.py:473
  239.1 40.8 %collective-permute-start.40 = (bf16[4,128,1024]{2,1,0:T(8,128)(2,1)S(1)}, bf16[4,128,1024]{2,1,0:T(8,128)(2,1)S(1)}, u32[]{:S(2)}, u32[]{:S(2)}) collective-permute-start(bf16[4,128,1024]{2,1,0:T(8,128)(2,1)S(1)} %get-tuple-element.146), channel_id=1, source_target_pairs={{0,16},{4,20},{8,24},{12,28},{16,0},{20,4},{24,8},{28,12},{1,17},{... | collective-permute-start | bytes 3145736 | tf_op jit(solution)/shard_map/ppermute | solution.py:473
  258.7 42.6 %collective-permute-start.32 = (bf16[256,1024]{1,0:T(8,128)(2,1)S(1)}, bf16[256,1024]{1,0:T(8,128)(2,1)S(1)}, u32[]{:S(2)}, u32[]{:S(2)}) collective-permute-start(bf16[256,1024]{1,0:T(8,128)(2,1)S(1)} %get-tuple-element.133), channel_id=1, source_target_pairs={{0,0},{8,1},{4,2},{12,3},{1,4},{9,5},{5,6},{13,7},{2,8},{10,9},{6,... | collective-permute-start | bytes 1572872 | tf_op jit(solution)/shard_map/ppermute | solution.py:1175
  259.4 43.4 %collective-permute-start.41 = (bf16[256,1024]{1,0:T(8,128)(2,1)S(1)}, bf16[256,1024]{1,0:T(8,128)(2,1)S(1)}, u32[]{:S(2)}, u32[]{:S(2)}) collective-permute-start(bf16[256,1024]{1,0:T(8,128)(2,1)S(1)} %get-tuple-element.154.a0), channel_id=1, source_target_pairs={{0,4},{4,0},{8,12},{12,8},{16,20},{20,16},{24,28},{28,24},{1,5},{5... | collective-permute-start | bytes 1572872 | tf_op jit(solution)/shard_map/ppermute | solution.py:473
  264.7 39.1 %collective-permute-start.42 = (bf16[256,1024]{1,0:T(8,128)(2,1)S(1)}, bf16[256,1024]{1,0:T(8,128)(2,1)S(1)}, u32[]{:S(2)}, u32[]{:S(2)}) collective-permute-start(bf16[256,1024]{1,0:T(8,128)(2,1)S(1)} %collective-permute-done.39.a1), channel_id=1, source_target_pairs={{0,4},{4,0},{8,12},{12,8},{16,20},{20,16},{24,28},{28,24},{1,5},{5... | collective-permute-start | bytes 1572872 | tf_op jit(solution)/shard_map/ppermute | solution.py:473
  294.7 29.6 %collective-permute-start.46 = (bf16[128,1024]{1,0:T(8,128)(2,1)S(1)}, bf16[128,1024]{1,0:T(8,128)(2,1)S(1)}, u32[]{:S(2)}, u32[]{:S(2)}) collective-permute-start(bf16[128,1024]{1,0:T(8,128)(2,1)S(1)} %get-tuple-element.156), channel_id=1, source_target_pairs={{0,1},{1,2},{2,3},{3,0},{4,5},{5,6},{6,7},{7,4},{8,9},{9,10},{10,1... | collective-permute-start | bytes 786440 | tf_op jit(solution)/shard_map/ppermute | solution.py:478
  297.8 26.5 %collective-permute-start.47 = (bf16[128,1024]{1,0:T(8,128)(2,1)S(1)}, bf16[128,1024]{1,0:T(8,128)(2,1)S(1)}, u32[]{:S(2)}, u32[]{:S(2)}) collective-permute-start(bf16[128,1024]{1,0:T(8,128)(2,1)S(1)} %get-tuple-element.157), channel_id=1, source_target_pairs={{0,2},{1,3},{2,0},{3,1},{4,6},{5,7},{6,4},{7,5},{8,10},{9,11},{10,... | collective-permute-start | bytes 786440 | tf_op jit(solution)/shard_map/ppermute | solution.py:478
  322.7 38.6 %collective-permute-start.50 = (bf16[4,128,1024]{2,1,0:T(8,128)(2,1)}, bf16[4,128,1024]{2,1,0:T(8,128)(2,1)}, u32[]{:S(2)}, u32[]{:S(2)}) collective-permute-start(bf16[4,128,1024]{2,1,0:T(8,128)(2,1)} %get-tuple-element.174), channel_id=1, source_target_pairs={{0,16},{4,20},{8,24},{12,28},{16,0},{20,4},{24,8},{28,12},{1,17},{... | collective-permute-start | bytes 3145736 | tf_op jit(solution)/shard_map/ppermute | solution.py:473
  325.6 34.6 %collective-permute-start.68 = (bf16[2,128,1024]{2,1,0:T(8,128)(2,1)S(1)}, bf16[2,128,1024]{2,1,0:T(8,128)(2,1)S(1)}, u32[]{:S(2)}, u32[]{:S(2)}) collective-permute-start(bf16[2,128,1024]{2,1,0:T(8,128)(2,1)S(1)} %pad_maximum_fusion.6), channel_id=1, source_target_pairs={{0,16},{4,20},{8,24},{12,28},{16,0},{20,4},{24,8},{28,12},{1,17},{... | collective-permute-start | bytes 1572872 | tf_op jit(solution)/shard_map/ppermute | solution.py:473
  332.5 37.1 %collective-permute-start.71 = (bf16[2,128,1024]{2,1,0:T(8,128)(2,1)}, bf16[2,128,1024]{2,1,0:T(8,128)(2,1)S(1)}, u32[]{:S(2)}, u32[]{:S(2)}) collective-permute-start(bf16[2,128,1024]{2,1,0:T(8,128)(2,1)} %pad_maximum_fusion.7), channel_id=1, source_target_pairs={{0,16},{4,20},{8,24},{12,28},{16,0},{20,4},{24,8},{28,12},{1,17},{... | collective-permute-start | bytes 1572872 | tf_op jit(solution)/shard_map/ppermute | solution.py:473
  333.0 51.4 %collective-permute-start.44 = (bf16[256,1024]{1,0:T(8,128)(2,1)}, bf16[256,1024]{1,0:T(8,128)(2,1)}, u32[]{:S(2)}, u32[]{:S(2)}) collective-permute-start(bf16[256,1024]{1,0:T(8,128)(2,1)} %get-tuple-element.170), channel_id=1, source_target_pairs={{0,4},{4,0},{8,12},{12,8},{16,20},{20,16},{24,28},{28,24},{1,5},{5... | collective-permute-start | bytes 1572872 | tf_op jit(solution)/shard_map/ppermute | solution.py:473
  369.6 34.7 %collective-permute-start.43 = (bf16[256,1024]{1,0:T(8,128)(2,1)}, bf16[256,1024]{1,0:T(8,128)(2,1)S(1)}, u32[]{:S(2)}, u32[]{:S(2)}) collective-permute-start(bf16[256,1024]{1,0:T(8,128)(2,1)} %copy-done.30), channel_id=1, source_target_pairs={{0,4},{4,0},{8,12},{12,8},{16,20},{20,16},{24,28},{28,24},{1,5},{5... | collective-permute-start | bytes 1572872 | tf_op jit(solution)/shard_map/ppermute | solution.py:473
  374.8 49.8 %collective-permute-start.69 = (bf16[4,128,1024]{2,1,0:T(8,128)(2,1)}, bf16[4,128,1024]{2,1,0:T(8,128)(2,1)}, u32[]{:S(2)}, u32[]{:S(2)}) collective-permute-start(bf16[4,128,1024]{2,1,0:T(8,128)(2,1)} %pad_maximum_fusion.1), channel_id=1, source_target_pairs={{0,4},{4,0},{8,12},{12,8},{16,20},{20,16},{24,28},{28,24},{1,5},{5... | collective-permute-start | bytes 3145736 | tf_op jit(solution)/shard_map/ppermute | solution.py:473
  382.3 44.7 %collective-permute-start.72 = (bf16[4,128,1024]{2,1,0:T(8,128)(2,1)}, bf16[4,128,1024]{2,1,0:T(8,128)(2,1)}, u32[]{:S(2)}, u32[]{:S(2)}) collective-permute-start(bf16[4,128,1024]{2,1,0:T(8,128)(2,1)} %pad_maximum_fusion.2), channel_id=1, source_target_pairs={{0,4},{4,0},{8,12},{12,8},{16,20},{20,16},{24,28},{28,24},{1,5},{5... | collective-permute-start | bytes 3145736 | tf_op jit(solution)/shard_map/ppermute | solution.py:473
  409.9 31.0 %collective-permute-start.56 = (bf16[4,128,1024]{2,1,0:T(8,128)(2,1)}, bf16[4,128,1024]{2,1,0:T(8,128)(2,1)}, u32[]{:S(2)}, u32[]{:S(2)}) collective-permute-start(bf16[4,128,1024]{2,1,0:T(8,128)(2,1)} %pad_maximum_fusion), channel_id=1, source_target_pairs={{0,4},{4,0},{8,12},{12,8},{16,20},{20,16},{24,28},{28,24},{1,5},{5... | collective-permute-start | bytes 3145736 | tf_op jit(solution)/shard_map/ppermute | solution.py:473
  412.9 25.9 %collective-permute-start.49 = (bf16[256,1024]{1,0:T(8,128)(2,1)}, bf16[256,1024]{1,0:T(8,128)(2,1)}, u32[]{:S(2)}, u32[]{:S(2)}) collective-permute-start(bf16[256,1024]{1,0:T(8,128)(2,1)} %get-tuple-element.177), channel_id=1, source_target_pairs={{0,0},{8,1},{4,2},{12,3},{1,4},{9,5},{5,6},{13,7},{2,8},{10,9},{6,... | collective-permute-start | bytes 1572872 | tf_op jit(solution)/shard_map/ppermute | solution.py:1238
  (83 other events, 1223.7 us)
